TPU v7x, 128 devices: a whole 4x4x4 slice. The times are simulated.
128 devices in a mesh: sub: 16 (over x_hi, z, core), sta: 8 (over x_lo, y).
Axes of the slice: x: 4 (x_hi: 2, x_lo: 2; x = x_hi * 2 + x_lo), y: 4, z: 4, core: 2. Of those that a mesh axis runs over, the one named last changes fastest.
Arguments:
- voltages: bfloat16 [16, 2, 64, 65536], P('sub', None, 'sta'), may hold values from -6 to 6
- beam_weights: bfloat16 [16, 2, 32, 64], P('sub'), may hold values from -0.5 to 0.5
- station_delays: int32 [64], P('sta'), may hold values from 0 to 16383
- dm_index: int32 [32, 1], P('sta'), may hold values from 1 to 8
Outputs:
- dedispersed: float32 [16, 2, 32, 1, 65536], P(None, None, None, None, ('sub', 'sta'))
- intensity: float32 [32, 1, 65536], P(None, None, ('sub', 'sta'))
Inputs may be any that keep to these rules, and one draw needn't show every extreme that they name: `station_delays`: delays in whole samples. `dm_index`: dispersion measure in steps of 10.
All inputs are finite; a program needn't handle non-finite values.
Results may differ from a plain program's by a relative error of at most 0.0006.
Values may be sent and summed in bfloat16 or wider, within the bound.
A program may use at most 320 MiB of HBM per device.

v0:
```python
import jax
import jax.numpy as jnp
from jax import lax
from jax.sharding import PartitionSpec as P

ROOT = 256


TWO_PI = 6.283185307179586
DISPERSION = 4148808000.0
DM_STEP = 10.0
BASE_FREQ = 120.0
CHANNEL_WIDTH = 0.1953125
HIGHEST = lax.Precision.HIGHEST


def in_blocks(array, dim, devices):
    shape = array.shape
    tiles = array.reshape(*shape[:dim], devices, shape[dim] // devices, *shape[dim + 1 :])
    return jnp.moveaxis(tiles, dim, 0)


def in_order(tiles, dim):
    shape = list(tiles.shape[1:])
    shape[dim] *= tiles.shape[0]
    return jnp.moveaxis(tiles, 0, dim).reshape(shape)


def joined_exchange(array, axis, axes, splits, concats):
    sizes = [lax.axis_size(a) for a in axes]
    tiles = in_blocks(array, splits[0], sizes[0])
    tiles = jnp.moveaxis(in_blocks(tiles, splits[1] + 1, sizes[1]), 0, 1)
    inside = tiles.shape[2:]
    tiles = tiles.reshape(-1, *inside)
    tiles = lax.all_to_all(tiles, axis, split_axis=0, concat_axis=0, tiled=True)
    tiles = in_order(tiles.reshape(*sizes, *inside), concats[0] + 1)
    return in_order(tiles, concats[1])


def angle_tables(rows_len, modulus):
    first = jnp.arange(rows_len, dtype=jnp.int32)[:, None]
    second = jnp.arange(rows_len, dtype=jnp.int32)[None, :]
    product = first * second % modulus
    angles = TWO_PI * product.astype(jnp.float32) / modulus
    return (jnp.cos(angles), jnp.sin(angles))


def chirp_base(subband, root_len, total_len):
    first = jnp.arange(root_len, dtype=jnp.int32)[:, None]
    second = jnp.arange(root_len, dtype=jnp.int32)[None, :]
    positions = first + root_len * second
    signed_bin = jnp.where(positions < total_len // 2, positions, positions - total_len)
    offset = (CHANNEL_WIDTH * signed_bin.astype(jnp.float32) / total_len)[None]
    centre = (BASE_FREQ + CHANNEL_WIDTH * (subband.astype(jnp.float32) + 0.5))[:, None, None]
    return TWO_PI * DISPERSION * offset * offset / (centre * centre * (centre + offset))


def left_dft(cos_table, sin_table, x_real, x_imag, flip_sign):
    real_part = jnp.einsum(
        "kt,...tu->...ku", cos_table, x_real, precision=HIGHEST
    ) + flip_sign * jnp.einsum("kt,...tu->...ku", sin_table, x_imag, precision=HIGHEST)
    imag_part = jnp.einsum(
        "kt,...tu->...ku", cos_table, x_imag, precision=HIGHEST
    ) - flip_sign * jnp.einsum("kt,...tu->...ku", sin_table, x_real, precision=HIGHEST)
    return (real_part, imag_part)


def right_dft(cos_table, sin_table, x_real, x_imag, flip_sign):
    real_part = jnp.einsum(
        "...kt,tm->...km", x_real, cos_table, precision=HIGHEST
    ) + flip_sign * jnp.einsum("...kt,tm->...km", x_imag, sin_table, precision=HIGHEST)
    imag_part = jnp.einsum(
        "...kt,tm->...km", x_imag, cos_table, precision=HIGHEST
    ) - flip_sign * jnp.einsum("...kt,tm->...km", x_real, sin_table, precision=HIGHEST)
    return (real_part, imag_part)


def beam_terms(w_block, v_real, v_imag):
    w_real = w_block[:, 0]
    w_imag = w_block[:, 1]
    real_part = jnp.einsum(
        "sbk,skt->bst", w_real, v_real, preferred_element_type=jnp.float32
    ) - jnp.einsum("sbk,skt->bst", w_imag, v_imag, preferred_element_type=jnp.float32)
    imag_part = jnp.einsum(
        "sbk,skt->bst", w_real, v_imag, preferred_element_type=jnp.float32
    ) + jnp.einsum("sbk,skt->bst", w_imag, v_real, preferred_element_type=jnp.float32)
    return jnp.stack([real_part, imag_part], axis=2)


def shards(voltages, beam_weights, station_delays, dm_index):
    sub_dev = voltages.shape[0]
    total_len = voltages.shape[3]
    local_beams = dm_index.shape[0]
    trials = dm_index.shape[1]
    root_len = ROOT
    doubled = jnp.concatenate([voltages, voltages], axis=3)
    shifted = jax.vmap(
        lambda rows, shift_by: lax.dynamic_slice_in_dim(rows, total_len - shift_by, total_len, 2),
        in_axes=(2, 0),
        out_axes=2,
    )(doubled, station_delays)
    own_weights = lax.dynamic_slice_in_dim(
        beam_weights, lax.axis_index("sta") * local_beams, local_beams, 2
    )
    shard_piece = lax.all_gather(shifted, "sta", axis=2, tiled=True)
    beams = beam_terms(own_weights, shard_piece[:, 0], shard_piece[:, 1])
    cos_root, sin_root = angle_tables(root_len, root_len)
    cos_twist, sin_twist = angle_tables(root_len, total_len)
    x_real = beams[:, :, 0].reshape(local_beams, sub_dev, root_len, root_len)
    x_imag = beams[:, :, 1].reshape(local_beams, sub_dev, root_len, root_len)
    a_real, a_imag = left_dft(cos_root, sin_root, x_real, x_imag, 1.0)
    b_real = a_real * cos_twist + a_imag * sin_twist
    b_imag = a_imag * cos_twist - a_real * sin_twist
    s_real, s_imag = right_dft(cos_root, sin_root, b_real, b_imag, 1.0)
    subband = lax.axis_index("sub") * sub_dev + jnp.arange(sub_dev, dtype=jnp.int32)
    base_phase = chirp_base(subband, root_len, total_len)
    dm_value = DM_STEP * dm_index.astype(jnp.float32)
    phase_table = dm_value[:, None, :, None, None] * base_phase[None, :, None, :, :]
    h_real = jnp.cos(phase_table)
    h_imag = jnp.sin(phase_table)
    c_real = s_real[:, :, None] * h_real - s_imag[:, :, None] * h_imag
    c_imag = s_real[:, :, None] * h_imag + s_imag[:, :, None] * h_real
    d_real, d_imag = right_dft(cos_root, sin_root, c_real, c_imag, -1.0)
    e_real = d_real * cos_twist - d_imag * sin_twist
    e_imag = d_imag * cos_twist + d_real * sin_twist
    scale = 1.0 / total_len
    out_real = jnp.einsum("tk,bsjku->sbjtu", cos_root, e_real, precision=HIGHEST) - jnp.einsum(
        "tk,bsjku->sbjtu", sin_root, e_imag, precision=HIGHEST
    )
    out_imag = jnp.einsum("tk,bsjku->sbjtu", cos_root, e_imag, precision=HIGHEST) + jnp.einsum(
        "tk,bsjku->sbjtu", sin_root, e_real, precision=HIGHEST
    )
    series = jnp.stack([out_real * scale, out_imag * scale], axis=1).reshape(
        sub_dev, 2, local_beams, trials, total_len
    )
    moved = joined_exchange(series, ("sub", "sta"), ("sub", "sta"), (4, 4), (0, 2))
    intensity = jnp.mean(moved[:, 0] * moved[:, 0] + moved[:, 1] * moved[:, 1], axis=0)
    return (moved, intensity)


def solution(mesh):
    return jax.shard_map(
        shards,
        mesh=mesh,
        in_specs=(
            P("sub", None, "sta", None),
            P("sub", None, None, None),
            P("sta"),
            P("sta", None),
        ),
        out_specs=(P(None, None, None, None, ("sub", "sta")), P(None, None, ("sub", "sta"))),
        check_vma=False,
    )
```

profile of v0, /device:TPU:0, one launch (start us, length us, event | category | flops | bytes accessed | tf_op | source)
XLA Modules:
  0.0 360.9 jit_solution(14308672278880408520)
XLA Ops:
  7.2 3.8 %copy.62 = bf16[1,2,8,65536]{3,1,0,2:T(2,128)(2,1)S(1)} copy(bf16[1,2,8,65536]{3,2,1,0:T(8,128)(2,1)} %param.4) | data formatting | bytes 4194304 | tf_op args[0]
  11.0 6.1 %maximum_bitcast_fusion = bf16[8,1,2,131072]{3,2,1,0:T(2,128)(2,1)} fusion(bf16[1,2,8,65536]{3,1,0,2:T(2,128)(2,1)S(1)} %copy.62), kind=kLoop, calls=%fused_computation.8 | loop fusion | flops 8388608 | bytes 6291456 | tf_op jit(solution)/shard_map/vmap()/transpose | solution.py:98
  17.1 31.3 %while.1 = (s32[]{:T(128)}, bf16[8,1,2,131072]{3,2,1,0:T(2,128)(2,1)}, s32[8,4]{0,1:T(4,128)S(1)}, bf16[8,1,2,65536]{3,2,1,0:T(2,128)(2,1)}, s32[]{:T(128)}) while((s32[]{:T(128)}, bf16[8,1,2,131072]{3,2,1,0:T(2,128)(2,1)}, s32[8,4]{0,1:T(4,128)S(1)}, bf16[8,1,2,65536]{3,2,1,0:T(2,128)(2,1)}, s32[]{:T(128)}) %tuple.26), condition=%wide.while_cond, body=%wide.while_body.sunk | while | flops 2 | bytes 525937 | solution.py:98
  17.8 3.2 dynamic-slice_dynamic-update-slice_fusion.2
  21.7 3.2 dynamic-slice_dynamic-update-slice_fusion.2
  25.6 3.2 dynamic-slice_dynamic-update-slice_fusion.2
  29.5 3.2 dynamic-slice_dynamic-update-slice_fusion.2
  33.3 3.2 dynamic-slice_dynamic-update-slice_fusion.2
  37.2 3.2 dynamic-slice_dynamic-update-slice_fusion.2
  41.1 3.2 dynamic-slice_dynamic-update-slice_fusion.2
  45.0 3.2 dynamic-slice_dynamic-update-slice_fusion.2
  48.4 4.1 %copy.119 = bf16[8,1,2,65536]{3,0,2,1:T(8,128)(2,1)} copy(bf16[8,1,2,65536]{3,2,1,0:T(2,128)(2,1)} %get-tuple-element.9) | data formatting | bytes 4194304 | tf_op jit(solution)/shard_map/vmap()/gather | solution.py:98
  54.0 171.7 %all-gather.2.cloned.1.call-done = bf16[1,2,64,65536]{3,2,1,0:T(8,128)(2,1)} async-done(((bf16[1,2,8,65536]{3,2,1,0:T(8,128)(2,1)}), bf16[1,2,64,65536]{3,2,1,0:T(8,128)(2,1)}) %all-gather.2.cloned.1.call-update) | async-done | bytes 16777232 | tf_op jit(solution)/shard_map/all_gather | solution.py:105
  225.7 4.7 %fusion.1 = f32[65536,4]{0,1:T(4,128)S(1)} fusion(bf16[1,2,64,65536]{3,2,1,0:T(8,128)(2,1)} %all-gather.2.cloned.1.call-done, bf16[1,2,32,64]{3,2,1,0:T(8,128)(2,1)S(1)} %copy-done, s32[]{:T(128)S(6)} %select_n.87), kind=kOutput, calls=%fused_computation.7 | convolution fusion | flops 33554432 | bytes 9438212 | tf_op jit(solution)/shard_map/sbk,skt->bst/dot_general | solution.py:84
  230.4 5.3 %convolution_add_fusion = f32[65536,4]{0,1:T(4,128)S(1)} fusion(f32[65536,4]{0,1:T(4,128)S(1)} %fusion.1, bf16[1,2,64,65536]{3,2,1,0:T(8,128)(2,1)} %all-gather.2.cloned.1.call-done, bf16[1,2,32,64]{3,2,1,0:T(8,128)(2,1)S(1)} %copy-done, s32[]{:T(128)S(6)} %add.214, s32[]{:T(128)S(6)} %select_n.87), kind=kOutput, calls=%fused_computation.2 | convolution fusion | flops 33816576 | bytes 10486792 | tf_op jit(solution)/shard_map/sbk,skt->bst/dot_general | solution.py:86
  240.9 2.9 fusion.20
  243.8 2.7 fusion.12
  246.5 2.7 fusion.13
  249.3 2.8 fusion.28
  252.0 2.8 fusion.24
  254.8 3.2 convolution_add_fusion.2
  258.0 2.8 convolution_subtract_fusion.2
  260.7 5.6 %fusion.51 = f32[4,256,256]{2,1,0:T(8,128)S(1)} fusion(f32[4,256,256]{2,1,0:T(8,128)S(1)} %convolution_add_fusion.2, f32[4,256,256]{2,1,0:T(8,128)S(1)} %convolution_subtract_fusion.2, f32[256,256]{1,0:T(8,128)S(1)} %multiply_divide_fusion, f32[4]{0:T(128)S(1)} %multiply_bitcast_fusion), kind=kOutput, calls=%fused_computation.83 | convolution fusion | flops 807272448 | bytes 3407888 | tf_op jit(solution)/shard_map/...kt,tm->...km/dot_general | solution.py:72
  266.4 5.8 %fusion.53 = f32[4,256,256]{2,1,0:T(8,128)S(1)} fusion(f32[4,256,256]{2,1,0:T(8,128)S(1)} %convolution_subtract_fusion.2, f32[4,256,256]{2,1,0:T(8,128)S(1)} %convolution_add_fusion.2, f32[256,256]{1,0:T(8,128)S(1)} %multiply_divide_fusion, f32[4]{0:T(128)S(1)} %multiply_bitcast_fusion), kind=kOutput, calls=%fused_computation.85 | convolution fusion | flops 807272448 | bytes 3407888 | tf_op jit(solution)/shard_map/...kt,tm->...km/dot_general | solution.py:69
  272.2 5.6 %fusion.10 = f32[4,256,256]{2,1,0:T(8,128)S(1)} fusion(f32[4,256,256]{2,1,0:T(8,128)S(1)} %fusion.51, f32[4,256,256]{2,1,0:T(8,128)S(1)} %convolution_subtract_fusion.2, f32[4,256,256]{2,1,0:T(8,128)S(1)} %convolution_add_fusion.2, f32[256,256]{1,0:T(8,128)S(1)} %multiply_divide_fusion, f32[4]{0:T(128)S(1)} %multiply_bitcast_fusion), kind=kOutput, calls=%fused_computation.25 | convolution fusion | flops 807796736 | bytes 4456464 | tf_op jit(solution)/shard_map/...kt,tm->...km/dot_general | solution.py:74
  277.8 5.9 %fusion.11 = f32[4,256,256]{2,1,0:T(8,128)S(1)} fusion(f32[4,256,256]{2,1,0:T(8,128)S(1)} %fusion.53, f32[4,256,256]{2,1,0:T(8,128)S(1)} %convolution_add_fusion.2, f32[4,256,256]{2,1,0:T(8,128)S(1)} %convolution_subtract_fusion.2, f32[256,256]{1,0:T(8,128)S(1)} %multiply_divide_fusion, f32[4]{0:T(128)S(1)} %multiply_bitcast_fusion), kind=kOutput, calls=%fused_computation.27 | convolution fusion | flops 807796736 | bytes 4456464 | tf_op jit(solution)/shard_map/...kt,tm->...km/dot_general | solution.py:71
  283.7 2.7 fusion.49
  286.5 3.7 %fusion.47 = f32[4,256,256]{2,1,0:T(8,128)} fusion(f32[4,256,256]{2,1,0:T(8,128)S(1)} %fusion.11, f32[4,256,256]{2,1,0:T(8,128)S(1)} %fusion.10, f32[256,256]{1,0:T(8,128)S(1)} %get-tuple-element.24, f32[256,256]{1,0:T(8,128)S(1)} %get-tuple-element.25), kind=kOutput, calls=%fused_computation.79 | convolution fusion | flops 807010304 | bytes 3670016 | tf_op jit(solution)/shard_map/tk,bsjku->sbjtu/dot_general | solution.py:130
  290.1 4.2 %fusion.9 = f32[1,4,1,256,256]{3,4,1,2,0:T(8,128)} fusion(f32[4,256,256]{2,1,0:T(8,128)S(1)} %fusion.49, f32[4,256,256]{2,1,0:T(8,128)S(1)} %fusion.11, f32[4,256,256]{2,1,0:T(8,128)S(1)} %fusion.10, f32[256,256]{1,0:T(8,128)S(1)} %get-tuple-element.24, f32[256,256]{1,0:T(8,128)S(1)} %get-tuple-element.25), kind=kOutput, calls=%fused_computation.23 | convolution fusion | flops 807534592 | bytes 4718592 | tf_op jit(solution)/shard_map/tk,bsjku->sbjtu/dot_general | solution.py:127
  299.3 4.9 %fusion.7 = f32[1,4,1,256,256]{3,4,1,2,0:T(8,128)} fusion(f32[4,256,256]{2,1,0:T(8,128)} %fusion.47, f32[4,256,256]{2,1,0:T(8,128)S(1)} %fusion.10, f32[4,256,256]{2,1,0:T(8,128)S(1)} %fusion.11, f32[256,256]{1,0:T(8,128)S(1)} %get-tuple-element.24, f32[256,256]{1,0:T(8,128)S(1)} %get-tuple-element.25), kind=kOutput, calls=%fused_computation.20 | convolution fusion | flops 807534592 | bytes 4718592 | tf_op jit(solution)/shard_map/tk,bsjku->sbjtu/dot_general | solution.py:130
  309.3 37.6 %all_to_all.5 = f32[128,1,2,4,1,512]{5,3,2,4,1,0:T(4,128)S(1)} all-to-all(f32[128,1,2,4,1,512]{5,3,2,4,1,0:T(4,128)S(1)} %bitcast.151), channel_id=1, replica_groups=mesh['sub'=16,'sta'=8] {'sub','sta'}, dimensions={0} | all-to-all | bytes 4194304 | tf_op jit(solution)/shard_map/all_to_all | solution.py:35
  349.4 3.5 copy.84
  (55 shorter events, 25.3 us)
Async XLA Ops:
  7.2 218.5 %copy-start = (bf16[1,2,32,64]{3,2,1,0:T(8,128)(2,1)S(1)}, bf16[1,2,32,64]{3,2,1,0:T(8,128)(2,1)}, u32[]{:S(2)}) copy-start(bf16[1,2,32,64]{3,2,1,0:T(8,128)(2,1)} %param.5) | copy-start | bytes 24580
  7.2 218.5 %all-gather.2.cloned.1.call-start = ((), (), s32[]{:S(2)}) async-start(), calls=%async_computation.1 | async-start | bytes 18874368 | tf_op jit(solution)/shard_map/all_gather | solution.py:105
  11.0 6.1 %copy-start.4 = (s32[8]{0:T(128)S(1)}, s32[8]{0:T(128)}, u32[]{:S(2)}) copy-start(s32[8]{0:T(128)} %param.6) | copy-start | bytes 100
  48.4 5.5 %copy-start.5 = (s32[4,1]{0,1:T(1,128)S(1)}, s32[4,1]{0,1:T(1,128)}, u32[]{:S(2)}) copy-start(s32[4,1]{0,1:T(1,128)} %param.7) | copy-start | bytes 52
  225.7 12.8 %copy-start.2 = (bf16[1,2,64,65536]{3,2,1,0:T(8,128)(2,1)S(1)}, bf16[1,2,64,65536]{3,2,1,0:T(8,128)(2,1)}, u32[]{:S(2)}) copy-start(bf16[1,2,64,65536]{3,2,1,0:T(8,128)(2,1)} %all-gather.2.cloned.1.call-done) | copy-start | bytes 50331652
  304.2 1.9 copy-start.3
  348.1 5.8 %copy-start.1 = (bf16[1,2,32,64]{3,2,1,0:T(8,128)(2,1)S(1)}, bf16[1,2,32,64]{3,2,1,0:T(8,128)(2,1)}, u32[]{:S(2)}) copy-start(bf16[1,2,32,64]{3,2,1,0:T(8,128)(2,1)} %param.5) | copy-start | bytes 24580
Sparse Core Ops, SparseCore 0:
  52.7 172.9 all-gather.1
where the time goes:
time: 367 us; the launch traced here: 361 us
  waiting for transfers between devices  172 us (47%)
  matrix products  73.4 us (20%)
  local copies, waits for them, and re-layouts  55.7 us (15%)
  blocking collectives  37.6 us (10%)
  between operations  14.5 us (4%)
  other arithmetic  7.77 us (2%)
    all_gather x1, waiting for transfers between devices, shards(): shard_piece = lax.all_gather(shifted, 'sta', axis=2, tiled=True)  172 us
    all_to_all x1, blocking collectives, joined_exchange(): tiles = lax.all_to_all(tiles, axis, split_axis=0, concat_axis=0, tiled=True)  37.6 us
    gather x24, local copies, waits for them, and re-layouts  31.1 us
    dot_general x2, matrix products, right_dft(): jnp.einsum('...kt,tm->...km', x_imag, sin_table, precision=HIGHEST)  9.03 us
    unnamed x16, local copies, waits for them, and re-layouts  8.91 us
    dot_general x2, matrix products, right_dft(): jnp.einsum('...kt,tm->...km', x_real, cos_table, precision=HIGHEST)  8.56 us
    dot_general x2, matrix products, right_dft(): jnp.einsum('...kt,tm->...km', x_real, sin_table, precision=HIGHEST)  8.4 us
    dot_general x2, matrix products, right_dft(): jnp.einsum('...kt,tm->...km', x_imag, cos_table, precision=HIGHEST)  8.39 us
  transfers between devices with their start and end apart: 1, of which 1 were waited for; matrix products, arithmetic and copies ran while one was open for 0% of the time, Pallas kernels for 0%

commit v1 on v0

v1 whole, which is shorter than its diff:
```python
import functools

import jax
import jax.numpy as jnp
import numpy as np
from jax import lax
from jax.experimental import pallas as pl
from jax.experimental.pallas import tpu as pltpu
from jax.sharding import PartitionSpec as P

TWO_PI = 6.283185307179586
DISPERSION = 4148808000.0
DM_STEP = 10.0
BASE_FREQ = 120.0
CHANNEL_WIDTH = 0.1953125
F32 = jnp.float32
BF16 = jnp.bfloat16
N = 65536
STA = 8
SUB = 16
INV_SQRT2 = 0.7071067811865476


def dft_tables():
    k = np.arange(128)
    ang = 2.0 * np.pi * ((k[:, None] * k[None, :]) % 128) / 128.0
    full = np.concatenate([np.cos(ang), np.sin(ang)], axis=1).astype(np.float32)
    hi = full.astype(jnp.bfloat16)
    lo = (full - hi.astype(np.float32)).astype(jnp.bfloat16)
    return np.concatenate([hi, hi], axis=0), lo


def twist_tables():
    ka = np.arange(64)[:, None]
    n = np.arange(1024)[None, :]
    ang = 2.0 * np.pi * (ka * n) / N
    big = np.stack([np.cos(ang), np.sin(ang)]).reshape(2, 64, 8, 128)
    kj = np.arange(8)[:, None]
    c = np.arange(128)[None, :]
    ang = 2.0 * np.pi * (kj * c) / 1024.0
    small = np.stack([np.cos(ang), np.sin(ang)])
    return big.astype(np.float32), small.astype(np.float32)


def chirp_base(subband):
    row = lax.broadcasted_iota(jnp.int32, (512, 128), 0)
    lane = lax.broadcasted_iota(jnp.int32, (512, 128), 1)
    positions = row + 512 * lane
    signed_bin = jnp.where(positions < N // 2, positions, positions - N)
    offset = CHANNEL_WIDTH * signed_bin.astype(F32) / N
    centre = BASE_FREQ + CHANNEL_WIDTH * (subband.astype(F32) + 0.5)
    return TWO_PI * DISPERSION * offset * offset / (centre * centre * (centre + offset))


def sign_rows():
    row = lax.broadcasted_iota(jnp.int32, (8, 128), 0)
    return jnp.where(row < 4, 1.0, -1.0).astype(F32)


def swap(x):
    return pltpu.roll(x, 4, x.ndim - 2)


def dft8(x, sg):
    def times_j(v):
        return swap(v) * sg

    def dft4(a0, a1, a2, a3):
        t0, t1, t2, t3 = a0 + a2, a0 - a2, a1 + a3, times_j(a1 - a3)
        return t0 + t2, t1 + t3, t0 - t2, t1 - t3

    e = dft4(x[0], x[2], x[4], x[6])
    o = dft4(x[1], x[3], x[5], x[7])
    j1, j3 = times_j(o[1]), times_j(o[3])
    o = (o[0], (o[1] + j1) * INV_SQRT2, times_j(o[2]), (j3 - o[3]) * INV_SQRT2)
    return [e[k] + o[k] for k in range(4)] + [e[k] - o[k] for k in range(4)]


def cmul(x, wr, wi, sg):
    return x * wr + (swap(x) * sg) * wi


def w64(a, k):
    ang = 2.0 * np.pi * ((a * k) % 64) / 64.0
    return float(np.cos(ang)), float(np.sin(ang))


def split(x):
    hi = x.astype(BF16)
    lo = (x - hi.astype(F32)).astype(BF16)
    return hi, lo


def unpack_voltages(x_ref, xf_ref):
    def body(i, _):
        for u in range(8):
            t = i * 8 + u
            col = pl.multiple_of(t * 128, 128)
            for ri in range(2):
                xf_ref[ri, t + 128] = x_ref[ri, :, pl.ds(col, 128)].astype(F32)
        return 0

    lax.fori_loop(0, 64, body, 0)

    def wrap(i, _):
        for u in range(8):
            for ri in range(2):
                xf_ref[ri, i * 8 + u] = xf_ref[ri, i * 8 + u + 512]
        return 0

    lax.fori_loop(0, 16, wrap, 0)


def delay_rows(d_ref, xf_ref, out_ref):
    row = lax.broadcasted_iota(jnp.int32, (8, 128), 0)
    lane = lax.broadcasted_iota(jnp.int32, (8, 128), 1)
    fine = jnp.zeros((8, 128), jnp.int32)
    starts = []
    for r in range(8):
        d = d_ref[r]
        starts.append(128 - d // 128)
        fine = jnp.where(row == r, d % 128, fine)
    masks = [row == r for r in range(8)]
    index = (lane - fine + 128) % 128
    keep = lane >= fine

    def gathered(ri, t):
        acc = xf_ref[ri, starts[0] + t]
        for r in range(1, 8):
            acc = jnp.where(masks[r], xf_ref[ri, starts[r] + t], acc)
        return jnp.take_along_axis(acc, index, axis=1)

    def body(a, carry):
        prev = list(carry)
        col = pl.multiple_of(a * 128, 128)
        for j in range(8):
            done = []
            for ri in range(2):
                now = gathered(ri, a * 8 + j)
                done.append(jnp.where(keep, now, prev[ri]))
                prev[ri] = now
            out_ref[j, :, pl.ds(col, 128)] = jnp.concatenate(done, axis=0).astype(BF16)
        return tuple(prev)

    lax.fori_loop(0, 64, body, (gathered(0, -1), gathered(1, -1)))


def p1_kernel(d_ref, x_ref, out_ref, xf_ref):
    unpack_voltages(x_ref, xf_ref)
    delay_rows(d_ref, xf_ref, out_ref)


def beamform(w_ref, v_ref, bm_ref):
    w = w_ref[...]

    def body(i, _):
        col = pl.multiple_of(i * 512, 512)
        v = v_ref[:, :, pl.ds(col, 512)].reshape(128, 512)
        out = jnp.dot(w, v, preferred_element_type=F32)
        for u in range(4):
            bm_ref[i * 4 + u] = out[:, u * 128 : (u + 1) * 128].reshape(8, 8, 128)
        return 0

    lax.fori_loop(0, 16, body, 0)


def dft64_forward(bm_ref, put, tiles, sg, twist, group=2):
    for a0 in range(8):

        def first(g, _):
            at = pl.ds(g * group, group)
            y = dft8([bm_ref[8 * a1 + a0, at] for a1 in range(8)], sg)
            for k0 in range(8):
                v = y[k0]
                if a0 * k0:
                    wr, wi = w64(a0, k0)
                    v = cmul(v, wr, wi, sg)
                bm_ref[8 * k0 + a0, at] = v
            return 0

        lax.fori_loop(0, tiles // group, first, 0)

    for k0 in range(8):

        def second(g, _):
            at = pl.ds(g * group, group)
            y = dft8([bm_ref[8 * k0 + a0, at] for a0 in range(8)], sg)
            for k1 in range(8):
                k = 8 * k1 + k0
                put(k, at, twist(k, y[k1]))
            return 0

        lax.fori_loop(0, tiles // group, second, 0)


def p2_kernel(w_ref, v_ref, tw_ref, out_ref, bm_ref):
    beamform(w_ref, v_ref, bm_ref)
    sg = sign_rows()

    def twist(k, v):
        return cmul(v, tw_ref[0, pl.ds(k, 1)], tw_ref[1, pl.ds(k, 1)], sg)

    def put(k, at, v):
        out_ref[at, k] = v

    dft64_forward(bm_ref, put, 8, sg, twist)


def chirp_table(dm_ref, base_ref, h_ref):
    row = lax.broadcasted_iota(jnp.int32, (8, 128), 0)
    quarter = jnp.where(row < 4, 1, 0)
    dm = dm_ref[...]
    p1 = 1.5703125
    p2 = float(np.float32(np.round((np.pi / 2 - p1) * 2.0**22) / 2.0**22))
    p3 = float(np.float32(np.pi / 2 - p1 - p2))

    def one(r):
        phase = dm * base_ref[pl.ds(r, 1), :]
        n = jnp.floor(phase * float(2.0 / np.pi) + 0.5)
        y = ((phase - n * p1) - n * p2) - n * p3
        q = n.astype(jnp.int32) + quarter
        z = y * y
        s = ((-1.9515295891e-4 * z + 8.3321608736e-3) * z - 1.6666654611e-1) * z * y + y
        c = ((2.443315711809948e-5 * z - 1.388731625493765e-3) * z + 4.166664568298827e-2) * z * z - 0.5 * z + 1.0
        v = jnp.where((q & 1) == 0, s, c)
        h_ref[r] = jnp.where((q & 2) == 0, v, -v)

    def body(i, _):
        for u in range(4):
            one(i * 4 + u)
        return 0

    lax.fori_loop(0, 128, body, 0)


def spectrum_and_back(r_ref, h_ref, w1_ref, w2_ref, tws_ref, twb_ref, out_put, xs_ref, g_ref):
    sg = sign_rows()

    def fwd(i, _):
        at = pl.ds(i * 2, 2)
        y = dft8([r_ref[j, at] for j in range(8)], sg)
        for kj in range(8):
            v = y[kj]
            if kj:
                v = cmul(v, tws_ref[0, pl.ds(kj, 1)], tws_ref[1, pl.ds(kj, 1)], sg)
            hi, lo = split(v.reshape(16, 128))
            at_rows = pl.ds(pl.multiple_of(kj * 512 + i * 16, 16), 16)
            xs_ref[at_rows, 0:128] = hi
            xs_ref[at_rows, 128:256] = lo
        return 0

    lax.fori_loop(0, 32, fwd, 0)

    rows = 128

    def dot128(at, sign):
        x = xs_ref[at, :]
        pq = jnp.dot(x, w1_ref[...], preferred_element_type=F32)
        pq = pq + jnp.dot(x[:, 0:128], w2_ref[...], preferred_element_type=F32)
        p = pq[:, 0:128].reshape(rows // 8, 8, 128)
        q = pq[:, 128:256].reshape(rows // 8, 8, 128)
        return p + swap(q) * sign

    low = lax.broadcasted_iota(jnp.int32, (8, 128), 0) < 4

    def mid(i, _):
        at = pl.ds(pl.multiple_of(i * rows, rows), rows)
        v = dot128(at, sg)
        h = h_ref[pl.ds(i * (rows // 8), rows // 8)]
        hs = swap(h)
        hr = jnp.where(low, h, hs)
        hi = jnp.where(low, -hs, h)
        v = v * hr + swap(v) * hi
        hi, lo = split(v.reshape(rows, 128))
        xs_ref[at, 0:128] = hi
        xs_ref[at, 128:256] = lo
        return 0

    lax.fori_loop(0, 4096 // rows, mid, 0)

    def back(i, _):
        at = pl.ds(pl.multiple_of(i * rows, rows), rows)
        v = dot128(at, -sg)
        per = 64 // (rows // 8)
        kj, part = i // per, i % per
        g_ref[pl.ds(part * (rows // 8), rows // 8), kj] = v
        return 0

    lax.fori_loop(0, 4096 // rows, back, 0)

    def inv8(ka, _):
        x = []
        for kj in range(8):
            v = g_ref[ka, kj]
            if kj:
                v = cmul(v, tws_ref[0, pl.ds(kj, 1)], tws_ref[1, pl.ds(kj, 1)], -sg)
            x.append(v)
        y = dft8(x, -sg)
        for j in range(8):
            g_ref[ka, j] = cmul(y[j], twb_ref[0, ka, pl.ds(j, 1)], twb_ref[1, ka, pl.ds(j, 1)], -sg)
        return 0

    lax.fori_loop(0, 64, inv8, 0, unroll=2)
    dft64_forward(g_ref, out_put, 8, -sg, lambda k, v: v * (1.0 / N))


def p3_kernel(r_ref, dm_ref, base_ref, w1_ref, w2_ref, tws_ref, twb_ref, out_ref, h_ref, xs_ref, g_ref):
    chirp_table(dm_ref, base_ref, h_ref)

    def put(a, at, v):
        out_ref[a, at] = v

    spectrum_and_back(r_ref, h_ref, w1_ref, w2_ref, tws_ref, twb_ref, put, xs_ref, g_ref)


def p4_kernel(r_ref, out_ref, int_ref):
    int_ref[...] = jnp.zeros_like(int_ref)

    def body(s, _):
        for sta in range(8):
            parts = []
            for ri in range(2):
                rows = [
                    r_ref[pl.ds((s * 8 + sta) * 32 + ri * 4 + b4, 4, stride=8), :] for b4 in range(4)
                ]
                block = jnp.concatenate(rows, axis=0)
                out_ref[pl.ds(pl.multiple_of(s * 256 + ri * 128 + sta * 16, 16), 16), :] = block
                parts.append(block)
            at = pl.ds(sta * 16, 16)
            int_ref[at, :] = int_ref[at, :] + (parts[0] * parts[0] + parts[1] * parts[1])
        return 0

    lax.fori_loop(0, 16, body, 0)
    int_ref[...] = int_ref[...] * (1.0 / SUB)


VM = pl.BlockSpec(memory_space=pltpu.VMEM)
SM = pl.BlockSpec(memory_space=pltpu.SMEM)
PARAMS = pltpu.CompilerParams(vmem_limit_bytes=60 * 1024 * 1024)


def p1(delays, volts):
    return pl.pallas_call(
        p1_kernel,
        out_shape=jax.ShapeDtypeStruct((8, 16, 8192), BF16),
        in_specs=[SM, VM],
        out_specs=VM,
        scratch_shapes=[pltpu.VMEM((2, 640, 8, 128), F32)],
        compiler_params=PARAMS,
    )(delays, volts)


def p2(w, v, tw):
    return pl.pallas_call(
        p2_kernel,
        out_shape=jax.ShapeDtypeStruct((8, 64, 8, 128), F32),
        in_specs=[VM, VM, VM],
        out_specs=VM,
        scratch_shapes=[pltpu.VMEM((64, 8, 8, 128), F32)],
        compiler_params=PARAMS,
    )(w, v, tw)


def p3(r, dm, base, w1, w2, tws, twb):
    return pl.pallas_call(
        p3_kernel,
        out_shape=jax.ShapeDtypeStruct((64, 8, 8, 128), F32),
        in_specs=[VM] * 7,
        out_specs=VM,
        scratch_shapes=[
            pltpu.VMEM((512, 8, 128), F32),
            pltpu.VMEM((4096, 256), BF16),
            pltpu.VMEM((64, 8, 8, 128), F32),
        ],
        compiler_params=PARAMS,
    )(r, dm, base, w1, w2, tws, twb)


def p4(r):
    return pl.pallas_call(
        p4_kernel,
        out_shape=(jax.ShapeDtypeStruct((4096, 128), F32), jax.ShapeDtypeStruct((128, 128), F32)),
        in_specs=[VM],
        out_specs=(VM, VM),
        compiler_params=PARAMS,
    )(r)


def stacked_weights(beam_weights):
    w0 = beam_weights[0, 0].reshape(8, 4, 8, 8)
    w1 = beam_weights[0, 1].reshape(8, 4, 8, 8)
    real = jnp.stack([w0, -w1], axis=3)
    imag = jnp.stack([w1, w0], axis=3)
    return jnp.stack([real, imag], axis=1).reshape(64, 128)


def shards(voltages, beam_weights, station_delays, dm_index):
    w1, w2 = dft_tables()
    big, small = twist_tables()
    send = p1(station_delays, voltages[0])
    v = lax.all_to_all(send, "sta", split_axis=0, concat_axis=0, tiled=True)
    own = lax.dynamic_index_in_dim(jnp.asarray(big), lax.axis_index("sta"), 2, keepdims=False)
    f = p2(stacked_weights(beam_weights), v, own)
    r = lax.all_to_all(f, "sta", split_axis=0, concat_axis=0, tiled=True)
    base = chirp_base(lax.axis_index("sub"))
    dm = DM_STEP * dm_index.astype(F32)
    dm = jnp.broadcast_to(jnp.concatenate([dm, dm], axis=0), (8, 128))
    y = p3(r, dm, base, jnp.asarray(w1), jnp.asarray(w2), jnp.asarray(small), jnp.asarray(big))
    z = lax.all_to_all(y.reshape(128, 32, 128), ("sub", "sta"), split_axis=0, concat_axis=0, tiled=True)
    out, power = p4(z.reshape(4096, 128))
    return out.reshape(16, 2, 32, 1, 512), power.reshape(32, 1, 512)


def solution(mesh):
    return jax.shard_map(
        shards,
        mesh=mesh,
        in_specs=(
            P("sub", None, "sta", None),
            P("sub", None, None, None),
            P("sta"),
            P("sta", None),
        ),
        out_specs=(P(None, None, None, None, ("sub", "sta")), P(None, None, ("sub", "sta"))),
        check_vma=False,
    )
```

time: 367 us -> 150 us (0.41); the launches traced: 361 us -> 149 us
  waiting for transfers between devices: 172 us -> 47.2 us
  matrix products: 73.4 us -> 0 us
  local copies, waits for them, and re-layouts: 55.7 us -> 5.47 us
  Pallas kernels: 0 us -> 44.4 us
  between operations: 14.5 us -> 0.7 us
  starting transfers between devices: 0.04 us -> 9.43 us
  other arithmetic: 7.77 us -> 2.15 us
    all_gather x1 -> x0, waiting for transfers between devices: 172 us -> none  [shards(): shard_piece = lax.all_gather(shifted, 'sta', axis=2, tiled=True)]
    dot_general x20 -> x0, matrix products: 73.4 us -> none  [the longest x2 9.03 us: right_dft(): jnp.einsum('...kt,tm->...km', x_imag, sin_table, precision=HIGHEST)]
    all_to_all x0 -> x2, waiting for transfers between devices: none -> 47.2 us  [the longest x1 25.3 us: shards(): r = lax.all_to_all(f, 'sta', split_axis=0, concat_axis=0, tiled=True)]
    pallas_call x0 -> x4, Pallas kernels: none -> 44.4 us  [the longest x1 22.7 us: p3(): pl.pallas_call(p3_kernel, out_shape=jax.ShapeDtypeStruct((64, 8, 8, 128),...]
    gather x25 -> x0, local copies, waits for them, and re-layouts: 35.2 us -> none
    all_to_all x0 -> x2, starting transfers between devices: none -> 9.43 us  [the longest x1 5.66 us: shards(): v = lax.all_to_all(send, 'sta', split_axis=0, concat_axis=0, tiled=True)]
    unnamed x16 -> x8, local copies, waits for them, and re-layouts: 8.91 us -> 1.9 us
    transpose x1 -> x0, other arithmetic: 6.08 us -> none  [shards(): lax.dynamic_slice_in_dim(rows, total_len - shift_by, total_len, 2)]
  transfers between devices with their start and end apart: 1 -> 2, of which waited for: 1 -> 2; matrix products, arithmetic and copies ran while one was open for 0% -> 3% of each run, Pallas kernels for 0% -> 0%
where the time goes in v1:
time: 150 us; the launch traced here: 149 us
  waiting for transfers between devices  47.2 us (31%)
  Pallas kernels  44.4 us (30%)
  blocking collectives  39.7 us (26%)
  starting transfers between devices  9.43 us (6%)
  local copies, waits for them, and re-layouts  5.47 us (4%)
  other arithmetic  2.15 us (1%)
    all_to_all x1, blocking collectives, shards(): lax.all_to_all(y.reshape(128, 32, 128), ('sub', 'sta'), split_axis=0, con...  39.7 us
    all_to_all x1, waiting for transfers between devices, shards(): r = lax.all_to_all(f, 'sta', split_axis=0, concat_axis=0, tiled=True)  25.3 us
    pallas_call x1, Pallas kernels, p3(): pl.pallas_call(p3_kernel, out_shape=jax.ShapeDtypeStruct((64, 8, 8, 128),...  22.7 us
    all_to_all x1, waiting for transfers between devices, shards(): v = lax.all_to_all(send, 'sta', split_axis=0, concat_axis=0, tiled=True)  21.9 us
    pallas_call x1, Pallas kernels, p1(): pl.pallas_call(p1_kernel, out_shape=jax.ShapeDtypeStruct((8, 16, 8192), B...  11.3 us
    pallas_call x1, Pallas kernels, p2(): pl.pallas_call(p2_kernel, out_shape=jax.ShapeDtypeStruct((8, 64, 8, 128),...  7.04 us
    all_to_all x1, starting transfers between devices, shards(): v = lax.all_to_all(send, 'sta', split_axis=0, concat_axis=0, tiled=True)  5.66 us
    all_to_all x1, starting transfers between devices, shards(): r = lax.all_to_all(f, 'sta', split_axis=0, concat_axis=0, tiled=True)  3.77 us
  transfers between devices with their start and end apart: 2, of which 2 were waited for; matrix products, arithmetic and copies ran while one was open for 3% of the time, Pallas kernels for 0%

profile of v1, /device:TPU:0, one launch (start us, length us, event | category | flops | bytes accessed | tf_op | source)
XLA Modules:
  0.0 149.1 jit_solution(18386253310294147449)
XLA Ops:
  0.6 11.3 %shard_map.95 = bf16[8,16,8192]{2,1,0:T(8,128)(2,1)} custom-call(s32[8]{0:T(128)} %d_ref.1, bf16[2,8,65536]{2,1,0:T(8,128)(2,1)} %bitcast.18), custom_call_target="tpu_custom_call" | custom-call | tf_op jit(solution)/shard_map/pallas_call | solution.py:343
  11.9 0.0 copy-start.2
  11.9 5.7 %all-to-all-start = ((bf16[8,16,8192]{2,1,0:T(8,128)(2,1)}), bf16[8,16,8192]{2,1,0:T(8,128)(2,1)S(1)}, u32[]{:S(2)}, u32[]{:S(2)}) async-start(bf16[8,16,8192]{2,1,0:T(8,128)(2,1)} %shard_map.95), calls=%async_computation | async-start | bytes 4194304 | tf_op jit(solution)/shard_map/all_to_all | solution.py:401
  17.6 0.0 copy-done.2
  17.6 0.1 reshape_squeeze.4
  17.7 0.1 neg.10
  17.9 0.1 stack_reshape_squeeze.6
  18.0 0.7 maximum_bitcast_fusion
  18.7 0.4 pad_maximum_fusion
  19.1 0.9 reshape.29.w_ref
  20.0 1.7 %constant_dynamic-slice_fusion = f32[2,64,1,128]{3,2,1,0:T(1,128)} fusion(f32[2,64,8,128]{3,2,1,0:T(8,128)} %constant.47.clone.twb_ref, s32[]{:T(128)S(6)} %select_n.10), kind=kLoop, calls=%fused_computation.9 | loop fusion | bytes 131076 | tf_op jit(solution)/shard_map/jit(dynamic_index_in_dim)/dynamic_slice | solution.py:402
  21.7 21.9 %all-to-all-done.v_ref = bf16[8,16,8192]{2,1,0:T(8,128)(2,1)S(1)} async-done(((bf16[8,16,8192]{2,1,0:T(8,128)(2,1)}), bf16[8,16,8192]{2,1,0:T(8,128)(2,1)S(1)}, u32[]{:S(2)}, u32[]{:S(2)}) %all-to-all-start) | async-done | bytes 2097184 | tf_op jit(solution)/shard_map/all_to_all | solution.py:401
  43.6 0.0 copy-start
  43.6 1.3 copy-done
  44.9 7.0 %shard_map.96 = f32[8,64,8,128]{3,2,1,0:T(8,128)} custom-call(bf16[64,128]{1,0:T(8,128)(2,1)} %reshape.29.w_ref, bf16[8,16,8192]{2,1,0:T(8,128)(2,1)} %copy-done, f32[2,64,128]{2,1,0:T(8,128)} %bitcast.19), custom_call_target="tpu_custom_call" | custom-call | tf_op jit(solution)/shard_map/pallas_call | solution.py:354
  52.0 0.0 copy-start.3
  52.0 3.8 %all-to-all-start.1 = ((f32[8,64,8,128]{3,2,1,0:T(8,128)}), f32[8,64,8,128]{3,2,1,0:T(8,128)S(1)}, u32[]{:S(2)}, u32[]{:S(2)}) async-start(f32[8,64,8,128]{3,2,1,0:T(8,128)} %shard_map.96), calls=%async_computation.1 | async-start | bytes 4194304 | tf_op jit(solution)/shard_map/all_to_all | solution.py:404
  55.7 0.0 copy-done.3
  55.7 0.1 maximum_bitcast_fusion.2
  55.8 0.8 multiply_divide_fusion.base_ref
  56.6 25.3 %all-to-all-done.1.r_ref = f32[8,64,8,128]{3,2,1,0:T(8,128)S(1)} async-done(((f32[8,64,8,128]{3,2,1,0:T(8,128)}), f32[8,64,8,128]{3,2,1,0:T(8,128)S(1)}, u32[]{:S(2)}, u32[]{:S(2)}) %all-to-all-start.1) | async-done | bytes 2097184 | tf_op jit(solution)/shard_map/all_to_all | solution.py:404
  81.9 0.0 copy-start.1
  81.9 0.7 broadcast_in_dim.8.dm_ref
  82.7 0.6 copy-done.1
  83.3 22.7 %shard_map.97 = f32[64,8,8,128]{3,2,1,0:T(8,128)} custom-call(f32[8,64,8,128]{3,2,1,0:T(8,128)} %copy-done.1, f32[8,128]{1,0:T(8,128)} %broadcast_in_dim.8.dm_ref, f32[512,128]{1,0:T(8,128)} %multiply_divide_fusion.base_ref, bf16[256,256]{1,0:T(8,128)(2,1)} %constant.48.clone.w1_ref, bf16[128,256]{1,0:T(8,128)(2,1)} %constant.49.clone.w2_ref, ...), custom_call_target="tpu_custom_call" | custom-call | tf_op jit(solution)/shard_map/pallas_call | solution.py:365
  105.9 39.7 %all_to_all.15 = f32[128,32,128]{2,1,0:T(8,128)} all-to-all(f32[128,32,128]{2,1,0:T(8,128)} %bitcast.16), channel_id=1, replica_groups=mesh['sub'=16,'sta'=8] {'sub','sta'}, dimensions={0} | all-to-all | bytes 4194304 | tf_op jit(solution)/shard_map/all_to_all | solution.py:409
  145.7 3.5 %shard_map.98 = (f32[4096,128]{1,0:T(8,128)}, f32[128,128]{1,0:T(8,128)}) custom-call(f32[4096,128]{1,0:T(8,128)} %bitcast.17), custom_call_target="tpu_custom_call" | custom-call | tf_op jit(solution)/shard_map/pallas_call | solution.py:380
  (3 shorter events, 0.0 us)
Async XLA Ops:
  11.9 5.7 %copy-start.2 = (bf16[1,2,32,64]{3,2,1,0:T(8,128)(2,1)S(1)}, bf16[1,2,32,64]{3,2,1,0:T(8,128)(2,1)}, u32[]{:S(2)}) copy-start(bf16[1,2,32,64]{3,2,1,0:T(8,128)(2,1)} %param.9) | copy-start | bytes 24580
  11.9 31.7 %all-to-all-start = ((bf16[8,16,8192]{2,1,0:T(8,128)(2,1)}), bf16[8,16,8192]{2,1,0:T(8,128)(2,1)S(1)}, u32[]{:S(2)}, u32[]{:S(2)}) async-start(bf16[8,16,8192]{2,1,0:T(8,128)(2,1)} %shard_map.95), calls=%async_computation | async-start | bytes 4194304 | tf_op jit(solution)/shard_map/all_to_all | solution.py:401
  43.6 1.3 copy-start
  52.0 3.8 %copy-start.3 = (s32[4,1]{0,1:T(1,128)S(1)}, s32[4,1]{0,1:T(1,128)}, u32[]{:S(2)}) copy-start(s32[4,1]{0,1:T(1,128)} %param.11) | copy-start | bytes 52
  52.0 30.0 %all-to-all-start.1 = ((f32[8,64,8,128]{3,2,1,0:T(8,128)}), f32[8,64,8,128]{3,2,1,0:T(8,128)S(1)}, u32[]{:S(2)}, u32[]{:S(2)}) async-start(f32[8,64,8,128]{3,2,1,0:T(8,128)} %shard_map.96), calls=%async_computation.1 | async-start | bytes 4194304 | tf_op jit(solution)/shard_map/all_to_all | solution.py:404
  81.9 1.3 copy-start.1

commit v2 on v1

v2 whole, which is shorter than its diff:
```python
import functools

import jax
import jax.numpy as jnp
import numpy as np
from jax import lax
from jax.experimental import pallas as pl
from jax.experimental.pallas import tpu as pltpu
from jax.sharding import PartitionSpec as P

TWO_PI = 6.283185307179586
DISPERSION = 4148808000.0
DM_STEP = 10.0
BASE_FREQ = 120.0
CHANNEL_WIDTH = 0.1953125
F32 = jnp.float32
BF16 = jnp.bfloat16
N = 65536
STA = 8
SUB = 16
INV_SQRT2 = 0.7071067811865476


MESH = pl.DeviceIdType.MESH
CH = 4


def dft_tables():
    k = np.arange(128)
    ang = 2.0 * np.pi * ((k[:, None] * k[None, :]) % 128) / 128.0
    full = np.concatenate([np.cos(ang), np.sin(ang)], axis=1).astype(np.float32)
    hi = full.astype(jnp.bfloat16)
    lo = (full - hi.astype(np.float32)).astype(jnp.bfloat16)
    return np.concatenate([hi, hi], axis=0), lo


def twist_tables():
    at = np.arange(64)
    ka = (8 * (at % 8) + at // 8)[:, None]
    n = np.arange(1024)[None, :]
    ang = 2.0 * np.pi * (ka * n) / N
    big = np.stack([np.cos(ang), np.sin(ang)]).reshape(2, 64, 8, 128)
    kj = np.arange(8)[:, None]
    c = np.arange(128)[None, :]
    ang = 2.0 * np.pi * (kj * c) / 1024.0
    small = np.stack([np.cos(ang), np.sin(ang)])
    e = np.arange(8)
    ang = 2.0 * np.pi * (e[:, None] * e[None, :]) / 64.0
    inner = np.stack([np.cos(ang), np.sin(ang)])[..., None] * np.ones(128)
    return big.astype(np.float32), small.astype(np.float32), inner.astype(np.float32)


def sign_rows():
    row = lax.broadcasted_iota(jnp.int32, (8, 128), 0)
    return jnp.where(row < 4, 1.0, -1.0).astype(F32)


def swap(x):
    return pltpu.roll(x, 4, x.ndim - 2)


def dft8(x, sg):
    def times_j(v):
        return swap(v) * sg

    def dft4(a0, a1, a2, a3):
        t0, t1, t2, t3 = a0 + a2, a0 - a2, a1 + a3, times_j(a1 - a3)
        return t0 + t2, t1 + t3, t0 - t2, t1 - t3

    e = dft4(x[0], x[2], x[4], x[6])
    o = dft4(x[1], x[3], x[5], x[7])
    j1, j3 = times_j(o[1]), times_j(o[3])
    o = (o[0], (o[1] + j1) * INV_SQRT2, times_j(o[2]), (j3 - o[3]) * INV_SQRT2)
    return [e[k] + o[k] for k in range(4)] + [e[k] - o[k] for k in range(4)]


def cmul(x, wr, wi, sg):
    return x * wr + (swap(x) * sg) * wi


def split(x):
    hi = x.astype(BF16)
    lo = (x - hi.astype(F32)).astype(BF16)
    return hi, lo


def unpack_voltages(x_ref, xf_ref):
    def body(i, _):
        for u in range(8):
            t = i * 8 + u
            col = pl.multiple_of(t * 128, 128)
            for ri in range(2):
                xf_ref[ri, t + 128] = x_ref[0, ri, :, pl.ds(col, 128)].astype(F32)
        return 0

    lax.fori_loop(0, 64, body, 0)

    def wrap(i, _):
        for ri in range(2):
            xf_ref[ri, pl.ds(i * 8, 8)] = xf_ref[ri, pl.ds(i * 8 + 512, 8)]
        return 0

    lax.fori_loop(0, 16, wrap, 0)


def delay_setup(d_ref):
    row = lax.broadcasted_iota(jnp.int32, (8, 128), 0)
    lane = lax.broadcasted_iota(jnp.int32, (8, 128), 1)
    fine = jnp.zeros((8, 128), jnp.int32)
    starts = []
    for r in range(8):
        d = d_ref[r]
        starts.append(128 - d // 128)
        fine = jnp.where(row == r, d % 128, fine)
    return starts, [row == r for r in range(8)], (lane - fine + 128) % 128, lane >= fine


def delay_rows(setup, xf_ref, out_ref, a0):
    starts, masks, index, keep = setup

    def body(a1, _):
        t = (8 * a1 + a0) * 8
        col = pl.multiple_of((8 * a0 + a1) * 128, 128)
        done = []
        for ri in range(2):
            acc = xf_ref[ri, pl.ds(starts[0] + t - 1, 9)]
            for r in range(1, 8):
                acc = jnp.where(masks[r], xf_ref[ri, pl.ds(starts[r] + t - 1, 9)], acc)
            g = [jnp.take_along_axis(acc[u], index, axis=1) for u in range(9)]
            done.append([jnp.where(keep, g[u + 1], g[u]) for u in range(8)])
        for j in range(8):
            out_ref[j, :, pl.ds(col, 128)] = jnp.concatenate([done[0][j], done[1][j]], axis=0).astype(BF16)
        return 0

    lax.fori_loop(0, 8, body, 0)


def one_hot(shape, hit):
    row = lax.broadcasted_iota(jnp.int32, shape, 0)
    col = lax.broadcasted_iota(jnp.int32, shape, 1)
    return jnp.where(hit(row, col), 1.0, 0.0).astype(BF16)


def stacked_weights(bw_ref):
    w0, w1 = bw_ref[0, 0], bw_ref[0, 1]
    to_real = one_hot((64, 128), lambda q, c: c == (q // 8) * 16 + q % 8)
    to_imag = one_hot((64, 128), lambda q, c: c == (q // 8) * 16 + 8 + q % 8)
    dot = functools.partial(jnp.dot, preferred_element_type=F32)
    real = (dot(w0, to_real) - dot(w1, to_imag)).astype(BF16)
    imag = (dot(w1, to_real) + dot(w0, to_imag)).astype(BF16)
    rows_real = one_hot((64, 32), lambda r, b: r == (b // 4) * 8 + b % 4)
    rows_imag = one_hot((64, 32), lambda r, b: r == (b // 4) * 8 + 4 + b % 4)
    return (dot(rows_real, real) + dot(rows_imag, imag)).astype(BF16)


def beamform(w_ref, v_ref, bm_ref, part):
    w = w_ref[...]

    def body(i, _):
        first = part * 16 + i * 4
        v = v_ref[:, :, pl.ds(pl.multiple_of(first * 128, 512), 512)].reshape(128, 512)
        out = jnp.dot(w, v, preferred_element_type=F32)
        for u in range(4):
            bm_ref[first + u] = out[:, u * 128 : (u + 1) * 128].reshape(8, 8, 128)
        return 0

    lax.fori_loop(0, 4, body, 0)


def inner_pass(ref, lead, twi_ref, sg):
    def body(g, _):
        at = pl.ds(g * 2, 2)
        y = dft8([ref[8 * lead + i, at] for i in range(8)], sg)
        for k in range(8):
            v = y[k]
            if k:
                v = cmul(v, twi_ref[0, lead, pl.ds(k, 1)], twi_ref[1, lead, pl.ds(k, 1)], sg)
            ref[8 * lead + k, at] = v
        return 0

    lax.fori_loop(0, 4, body, 0)


def outer_pass(ref, tail, sg, put):
    def body(g, _):
        at = pl.ds(g * 2, 2)
        y = dft8([ref[8 * i + tail, at] for i in range(8)], sg)
        for k in range(8):
            put(k, g, y[k])
        return 0

    lax.fori_loop(0, 4, body, 0)


def chirp_table(dm_ref, base_ref, h_ref):
    row = lax.broadcasted_iota(jnp.int32, (8, 128), 0)
    lane = lax.broadcasted_iota(jnp.int32, (8, 128), 1)
    centre = BASE_FREQ + CHANNEL_WIDTH * (
        jnp.zeros((8, 128), F32) + lax.axis_index("sub").astype(F32) + 0.5
    )

    def base(i, _):
        part, kj, low = i // 16, (i // 2) % 8, i % 2
        positions = 8 * row + (2 * part + low) + 64 * kj + 512 * lane
        signed_bin = jnp.where(positions < N // 2, positions, positions - N)
        offset = CHANNEL_WIDTH * signed_bin.astype(F32) / N
        base_ref[pl.ds(pl.multiple_of(i * 8, 8), 8), :] = (
            TWO_PI * DISPERSION * offset * offset / (centre * centre * (centre + offset))
        )
        return 0

    lax.fori_loop(0, 64, base, 0)
    quarter = jnp.where(row < 4, 1, 0)
    dm = jnp.zeros((8, 128), F32)
    for b in range(4):
        dm = jnp.where(row % 4 == b, DM_STEP * dm_ref[b, 0].astype(F32), dm)
    p1 = 1.5703125
    p2 = float(np.float32(np.round((np.pi / 2 - p1) * 2.0**22) / 2.0**22))
    p3 = float(np.float32(np.pi / 2 - p1 - p2))

    def one(r):
        phase = dm * base_ref[pl.ds(r, 1), :]
        n = jnp.floor(phase * float(2.0 / np.pi) + 0.5)
        y = ((phase - n * p1) - n * p2) - n * p3
        q = n.astype(jnp.int32) + quarter
        z = y * y
        s = ((-1.9515295891e-4 * z + 8.3321608736e-3) * z - 1.6666654611e-1) * z * y + y
        c = ((2.443315711809948e-5 * z - 1.388731625493765e-3) * z + 4.166664568298827e-2) * z * z - 0.5 * z + 1.0
        v = jnp.where((q & 1) == 0, s, c)
        h_ref[r] = jnp.where((q & 2) == 0, v, -v)

    def body(i, _):
        for u in range(4):
            one(i * 4 + u)
        return 0

    lax.fori_loop(0, 128, body, 0)


def middle(p, r_ref, h_ref, w1_ref, w2_ref, tws_ref, twb_ref, xs_ref, gt_ref, g_ref, sg):
    def fwd(i, _):
        at = pl.ds(p * 16 + i * 2, 2)
        y = dft8([r_ref[j, at] for j in range(8)], sg)
        for kj in range(8):
            v = y[kj]
            if kj:
                v = cmul(v, tws_ref[0, pl.ds(kj, 1)], tws_ref[1, pl.ds(kj, 1)], sg)
            hi, lo = split(v.reshape(16, 128))
            rows = pl.ds(pl.multiple_of(kj * 128 + i * 16, 16), 16)
            xs_ref[rows, 0:128] = hi
            xs_ref[rows, 128:256] = lo
        return 0

    lax.fori_loop(0, 8, fwd, 0)

    def dot128(at, sign):
        x = xs_ref[at, :]
        pq = jnp.dot(x, w1_ref[...], preferred_element_type=F32)
        pq = pq + jnp.dot(x[:, 0:128], w2_ref[...], preferred_element_type=F32)
        return pq[:, 0:128].reshape(16, 8, 128) + swap(pq[:, 128:256].reshape(16, 8, 128)) * sign

    low = lax.broadcasted_iota(jnp.int32, (8, 128), 0) < 4

    def mid(kj, _):
        at = pl.ds(pl.multiple_of(kj * 128, 128), 128)
        v = dot128(at, sg)
        h = h_ref[pl.ds(p * 128 + kj * 16, 16)]
        hs = swap(h)
        v = v * jnp.where(low, h, hs) + swap(v) * jnp.where(low, -hs, h)
        hi, lo = split(v.reshape(128, 128))
        xs_ref[at, 0:128] = hi
        xs_ref[at, 128:256] = lo
        return 0

    lax.fori_loop(0, 8, mid, 0)

    def back(kj, _):
        gt_ref[kj] = dot128(pl.ds(pl.multiple_of(kj * 128, 128), 128), -sg)
        return 0

    lax.fori_loop(0, 8, back, 0)

    def inv8(i, _):
        at = pl.ds(i * 2, 2)
        x = []
        for kj in range(8):
            v = gt_ref[kj, at]
            if kj:
                v = cmul(v, tws_ref[0, pl.ds(kj, 1)], tws_ref[1, pl.ds(kj, 1)], -sg)
            x.append(v)
        y = dft8(x, -sg)
        here = pl.ds(p * 16 + i * 2, 2)
        for j in range(8):
            g_ref[here, j] = cmul(y[j], twb_ref[0, here, pl.ds(j, 1)], twb_ref[1, here, pl.ds(j, 1)], -sg)
        return 0

    lax.fori_loop(0, 8, inv8, 0)


def kernel(
    d_ref, dm_ref, x_hbm, bw_ref, w1_hbm, w2_hbm, tws_hbm, twb_hbm, twi_hbm,
    recv3,
    x_ref, w1_ref, w2_ref, tws_ref, twb_ref, twi_ref,
    xf_ref, send1, recv1, w_ref, bm_ref, send2, recv2, base_ref, h_ref, xs_ref, gt_ref, g_ref, send3,
    load_sem, sem1, rsem1, sem2, rsem2, sem3, rsem3,
):
    sub, sta = lax.axis_index("sub"), lax.axis_index("sta")
    me = sub * STA + sta

    x_load = pltpu.make_async_copy(x_hbm, x_ref, load_sem.at[0])
    x_load.start()
    tables = [
        pltpu.make_async_copy(a, b, load_sem.at[1 + i])
        for i, (a, b) in enumerate(
            [(w1_hbm, w1_ref), (w2_hbm, w2_ref), (tws_hbm, tws_ref), (twb_hbm, twb_ref), (twi_hbm, twi_ref)]
        )
    ]
    for t in tables:
        t.start()

    barrier = pltpu.get_barrier_semaphore()

    def greet(i, _):
        d = (me + i) % (SUB * STA)
        pl.semaphore_signal(barrier, inc=1, device_id={"sub": d // STA, "sta": d % STA}, device_id_type=MESH)
        return 0

    lax.fori_loop(1, SUB * STA, greet, 0)
    x_load.wait()
    unpack_voltages(x_ref, xf_ref)
    setup = delay_setup(d_ref)

    for part in range(CH):
        delay_rows(setup, xf_ref, send1, 2 * part)
        delay_rows(setup, xf_ref, send1, 2 * part + 1)
        if part == 0:
            pl.semaphore_wait(barrier, SUB * STA - 1)
        cols = pl.ds(part * 2048, 2048)

        def go1(i, _):
            d = (sta + i) % STA
            pltpu.make_async_remote_copy(
                src_ref=send1.at[d, :, cols],
                dst_ref=recv1.at[sta, :, cols],
                send_sem=sem1,
                recv_sem=rsem1.at[part],
                device_id={"sub": sub, "sta": d},
                device_id_type=MESH,
            ).start()
            return 0

        lax.fori_loop(1, STA, go1, 0)
        pltpu.make_async_copy(send1.at[sta, :, cols], recv1.at[sta, :, cols], rsem1.at[part]).start()

    w_ref[...] = stacked_weights(bw_ref)
    chirp_table(dm_ref, base_ref, h_ref)
    for t in tables:
        t.wait()
    sg = sign_rows()

    for part in range(CH):
        cols = pl.ds(part * 2048, 2048)
        pltpu.make_async_copy(recv1.at[:, :, cols], recv1.at[:, :, cols], rsem1.at[part]).wait()
        beamform(w_ref, recv1, bm_ref, part)
        inner_pass(bm_ref, 2 * part, twi_ref, sg)
        inner_pass(bm_ref, 2 * part + 1, twi_ref, sg)

    for part in range(CH):

        def step(low, _):
            k0 = 2 * part + low

            def put(k1, g, v):
                k = 8 * k0 + k1
                v = cmul(v, twb_ref[0, k, pl.ds(sta, 1)], twb_ref[1, k, pl.ds(sta, 1)], sg)
                send2[pl.ds(2 * g, 2), k] = v

            outer_pass(bm_ref, k0, sg, put)
            return 0

        lax.fori_loop(0, 2, step, 0)
        rows = pl.ds(part * 16, 16)

        def go2(i, _):
            d = (sta + i) % STA
            pltpu.make_async_remote_copy(
                src_ref=send2.at[d, rows],
                dst_ref=recv2.at[sta, rows],
                send_sem=sem2,
                recv_sem=rsem2.at[part],
                device_id={"sub": sub, "sta": d},
                device_id_type=MESH,
            ).start()
            return 0

        lax.fori_loop(1, STA, go2, 0)
        pltpu.make_async_copy(send2.at[sta, rows], recv2.at[sta, rows], rsem2.at[part]).start()

    for part in range(CH):
        rows = pl.ds(part * 16, 16)
        pltpu.make_async_copy(recv2.at[:, rows], recv2.at[:, rows], rsem2.at[part]).wait()
        middle(part, recv2, h_ref, w1_ref, w2_ref, tws_ref, twb_ref, xs_ref, gt_ref, g_ref, sg)
        inner_pass(g_ref, 2 * part, twi_ref, -sg)
        inner_pass(g_ref, 2 * part + 1, twi_ref, -sg)

    def group(i, _):
        a0 = (sta + i) % 8
        for g in range(4):
            y = dft8([g_ref[8 * k0 + a0, pl.ds(2 * g, 2)] for k0 in range(8)], -sg)
            for a1 in range(8):
                send3[2 * (8 * a1 + a0) + g // 2, pl.ds(2 * (g % 2), 2)] = y[a1] * (1.0 / N)

        def go3(n, _):
            d = (16 * (n // 2 + sub // 2) + 2 * a0 + n % 2) % (SUB * STA)

            @pl.when(d != me)
            def _():
                pltpu.make_async_remote_copy(
                    src_ref=send3.at[d],
                    dst_ref=recv3.at[me],
                    send_sem=sem3,
                    recv_sem=rsem3.at[sub],
                    device_id={"sub": d // STA, "sta": d % STA},
                    device_id_type=MESH,
                ).start()

            @pl.when(d == me)
            def _():
                pltpu.make_async_copy(send3.at[me], recv3.at[me], rsem3.at[sub]).start()

            return 0

        lax.fori_loop(0, 16, go3, 0)
        return 0

    lax.fori_loop(0, 8, group, 0)

    for s in range(SUB):
        block = recv3.at[pl.ds(s * STA, STA)]
        pltpu.make_async_copy(block, block, rsem3.at[s]).wait()
    others = pl.ds(0, STA - 1)
    pltpu.make_async_copy(send1.at[others], send1.at[others], sem1).wait()
    pltpu.make_async_copy(send2.at[others], send2.at[others], sem2).wait()
    others = pl.ds(0, SUB * STA - 1)
    pltpu.make_async_copy(send3.at[others], send3.at[others], sem3).wait()


def assemble(r_ref, out_ref, int_ref):
    s = pl.program_id(0)

    @pl.when(s == 0)
    def _():
        int_ref[...] = jnp.zeros_like(int_ref)

    for sta in range(STA):
        parts = []
        for ri in range(2):
            rows = [r_ref[pl.ds(sta * 32 + ri * 4 + b4, 4, stride=8), :] for b4 in range(4)]
            block = jnp.concatenate(rows, axis=0)
            out_ref[pl.ds(ri * 128 + sta * 16, 16), :] = block
            parts.append(block)
        at = pl.ds(sta * 16, 16)
        int_ref[at, :] += (parts[0] * parts[0] + parts[1] * parts[1]) * (1.0 / SUB)


VM = pl.BlockSpec(memory_space=pltpu.VMEM)
SM = pl.BlockSpec(memory_space=pltpu.SMEM)
ANY = pl.BlockSpec(memory_space=pl.ANY)


def shards(voltages, beam_weights, station_delays, dm_index):
    w1, w2 = dft_tables()
    big, small, inner = twist_tables()
    moved = pl.pallas_call(
        kernel,
        out_shape=jax.ShapeDtypeStruct((128, 4, 8, 128), F32),
        in_specs=[SM, SM, ANY, VM, ANY, ANY, ANY, ANY, ANY],
        out_specs=ANY,
        scratch_shapes=[
            pltpu.VMEM((1, 2, 8, N), BF16),
            pltpu.VMEM((256, 256), BF16),
            pltpu.VMEM((128, 256), BF16),
            pltpu.VMEM((2, 8, 128), F32),
            pltpu.VMEM((2, 64, 8, 128), F32),
            pltpu.VMEM((2, 8, 8, 128), F32),
            pltpu.VMEM((2, 640, 8, 128), F32),
            pltpu.VMEM((8, 16, 8192), BF16),
            pltpu.VMEM((8, 16, 8192), BF16),
            pltpu.VMEM((64, 128), BF16),
            pltpu.VMEM((64, 8, 8, 128), F32),
            pltpu.VMEM((8, 64, 8, 128), F32),
            pltpu.VMEM((8, 64, 8, 128), F32),
            pltpu.VMEM((512, 128), F32),
            pltpu.VMEM((512, 8, 128), F32),
            pltpu.VMEM((1024, 256), BF16),
            pltpu.VMEM((8, 16, 8, 128), F32),
            pltpu.VMEM((64, 8, 8, 128), F32),
            pltpu.VMEM((128, 4, 8, 128), F32),
            pltpu.SemaphoreType.DMA((6,)),
            pltpu.SemaphoreType.DMA,
            pltpu.SemaphoreType.DMA((CH,)),
            pltpu.SemaphoreType.DMA,
            pltpu.SemaphoreType.DMA((CH,)),
            pltpu.SemaphoreType.DMA,
            pltpu.SemaphoreType.DMA((SUB,)),
        ],
        compiler_params=pltpu.CompilerParams(
            collective_id=0, has_side_effects=True, vmem_limit_bytes=60 * 1024 * 1024
        ),
    )(
        station_delays, dm_index, voltages, beam_weights,
        jnp.asarray(w1), jnp.asarray(w2), jnp.asarray(small), jnp.asarray(big), jnp.asarray(inner),
    )
    out, power = pl.pallas_call(
        assemble,
        grid=(SUB,),
        out_shape=(jax.ShapeDtypeStruct((4096, 128), F32), jax.ShapeDtypeStruct((128, 128), F32)),
        in_specs=[pl.BlockSpec((256, 128), lambda s: (s, 0))],
        out_specs=(pl.BlockSpec((256, 128), lambda s: (s, 0)), pl.BlockSpec((128, 128), lambda s: (0, 0))),
        compiler_params=pltpu.CompilerParams(dimension_semantics=("arbitrary",)),
    )(moved.reshape(4096, 128))
    return out.reshape(16, 2, 32, 1, 512), power.reshape(32, 1, 512)


def solution(mesh):
    return jax.shard_map(
        shards,
        mesh=mesh,
        in_specs=(
            P("sub", None, "sta", None),
            P("sub", None, None, None),
            P("sta"),
            P("sta", None),
        ),
        out_specs=(P(None, None, None, None, ("sub", "sta")), P(None, None, ("sub", "sta"))),
        check_vma=False,
    )
```

time: 150 us -> 106 us (0.71)
  Pallas kernels: 44.4 us -> 103 us
  waiting for transfers between devices: 47.2 us -> 0 us
  blocking collectives: 39.7 us -> 0 us
  starting transfers between devices: 9.43 us -> 0 us
  local copies, waits for them, and re-layouts: 5.47 us -> 1.31 us
  other arithmetic: 2.15 us -> 0 us
    pallas_call x4 -> x2, Pallas kernels: 44.4 us -> 103 us  [the longest x1 93.4 us: shards(): pl.pallas_call(kernel, out_shape=jax.ShapeDtypeStruct((128, 4, 8, 128), F...]
    all_to_all x2 -> x0, waiting for transfers between devices: 47.2 us -> none  [the longest x1 25.3 us: shards(): r = lax.all_to_all(f, 'sta', split_axis=0, concat_axis=0, tiled=True)]
    all_to_all x1 -> x0, blocking collectives: 39.7 us -> none  [shards(): lax.all_to_all(y.reshape(128, 32, 128), ('sub', 'sta'), split_axis=0, con...]
    all_to_all x2 -> x0, starting transfers between devices: 9.43 us -> none  [the longest x1 5.66 us: shards(): v = lax.all_to_all(send, 'sta', split_axis=0, concat_axis=0, tiled=True)]
    dynamic_slice x1 -> x0, local copies, waits for them, and re-layouts: 1.72 us -> none  [shards(): lax.dynamic_index_in_dim(jnp.asarray(big), lax.axis_index('sta'), 2, keep...]
  transfers between devices with their start and end apart: 2 -> 0, of which waited for: 2 -> 0; matrix products, arithmetic and copies ran while one was open for 3% -> 0% of each run, Pallas kernels for 0% -> 0%
where the time goes in v2:
time: 106 us; the launch traced here: 105 us
  Pallas kernels  103 us (97%)
  local copies, waits for them, and re-layouts  1.31 us (1%)
    pallas_call x1, Pallas kernels, shards(): pl.pallas_call(kernel, out_shape=jax.ShapeDtypeStruct((128, 4, 8, 128), F...  93.4 us
    pallas_call x1, Pallas kernels, shards(): pl.pallas_call(assemble, grid=(SUB,), out_shape=(jax.ShapeDtypeStruct((40...  9.64 us

profile of v2, /device:TPU:0, one launch (start us, length us, event | category | flops | bytes accessed | tf_op | source)
XLA Modules:
  0.0 105.0 jit_solution(3450044788778274764)
XLA Ops:
  0.6 1.3 %copy.11.dm_ref = s32[4,1]{1,0:T(4,128)} copy(s32[4,1]{0,1:T(1,128)} %param.12) | data formatting | bytes 32 | tf_op args[3]
  1.9 93.4 %shard_map.104 = f32[128,4,8,128]{3,2,1,0:T(8,128)} custom-call(s32[8]{0:T(128)} %d_ref.1, s32[4,1]{1,0:T(4,128)} %copy.11.dm_ref, bf16[1,2,8,65536]{3,2,1,0:T(8,128)(2,1)} %x_hbm.1, bf16[1,2,32,64]{3,2,1,0:T(8,128)(2,1)} %bw_ref.1, bf16[256,256]{1,0:T(8,128)(2,1)} %constant.10.clone.w1_hbm, bf16[128,256]{1,0:T(8,128)(2,1)} %constant.11.clone.w2_hbm, ...), custom_call_target="tpu_custom_call" | custom-call | tf_op jit(solution)/shard_map/pallas_call | solution.py:474
  95.3 9.6 %shard_map.105 = (f32[4096,128]{1,0:T(8,128)}, f32[128,128]{1,0:T(8,128)}) custom-call(f32[4096,128]{1,0:T(8,128)} %bitcast.3), custom_call_target="tpu_custom_call" | custom-call | tf_op jit(solution)/shard_map/pallas_call | solution.py:514

commit v3 on v2

--- a/solution.py
+++ b/solution.py
@@ -22,6 +22,7 @@
 
 
 MESH = pl.DeviceIdType.MESH
+TOP = 32767.0
 CH = 4
 
 
@@ -178,18 +179,32 @@
             ref[8 * lead + k, at] = v
         return 0
 
-    lax.fori_loop(0, 4, body, 0)
-
-
-def outer_pass(ref, tail, sg, put):
-    def body(g, _):
-        at = pl.ds(g * 2, 2)
-        y = dft8([ref[8 * i + tail, at] for i in range(8)], sg)
-        for k in range(8):
-            put(k, g, y[k])
-        return 0
-
-    lax.fori_loop(0, 4, body, 0)
+    lax.fori_loop(0, 4, body, 0, unroll=4)
+
+
+def encode(values, axes):
+    top = jnp.max(jnp.abs(values), axis=axes, keepdims=True)
+    top = jnp.maximum(top, 1e-33)
+    return jnp.round(values * (TOP / top)), top * (1.0 / TOP)
+
+
+def decode(ints):
+    return ints.astype(jnp.int32).astype(F32)
+
+
+def outer_and_encode(bm_ref, part, sta, twb_ref, sg, q_ref, s_ref):
+    for low in range(2):
+        k0 = 2 * part + low
+        for g in range(4):
+            at = pl.ds(2 * g, 2)
+            y = dft8([bm_ref[8 * i + k0, at] for i in range(8)], sg)
+            out = []
+            for k1 in range(8):
+                k = 8 * k0 + k1
+                out.append(cmul(y[k1], twb_ref[0, k, pl.ds(sta, 1)], twb_ref[1, k, pl.ds(sta, 1)], sg))
+            q, scale = encode(jnp.stack(out, axis=1), (1, 2))
+            q_ref[at, pl.ds(4 * k0, 4)] = q.reshape(2, 4, 16, 128).astype(jnp.int16)
+            s_ref[at, part, low : low + 1] = scale.reshape(2, 1, 128)
 
 
 def chirp_table(dm_ref, base_ref, h_ref):
@@ -213,7 +228,7 @@
     quarter = jnp.where(row < 4, 1, 0)
     dm = jnp.zeros((8, 128), F32)
     for b in range(4):
-        dm = jnp.where(row % 4 == b, DM_STEP * dm_ref[b, 0].astype(F32), dm)
+        dm = jnp.where(row % 4 == b, DM_STEP * dm_ref[b].astype(F32), dm)
     p1 = 1.5703125
     p2 = float(np.float32(np.round((np.pi / 2 - p1) * 2.0**22) / 2.0**22))
     p3 = float(np.float32(np.pi / 2 - p1 - p2))
@@ -237,48 +252,56 @@
     lax.fori_loop(0, 128, body, 0)
 
 
-def middle(p, r_ref, h_ref, w1_ref, w2_ref, tws_ref, twb_ref, xs_ref, gt_ref, g_ref, sg):
-    def fwd(i, _):
-        at = pl.ds(p * 16 + i * 2, 2)
-        y = dft8([r_ref[j, at] for j in range(8)], sg)
-        for kj in range(8):
-            v = y[kj]
-            if kj:
-                v = cmul(v, tws_ref[0, pl.ds(kj, 1)], tws_ref[1, pl.ds(kj, 1)], sg)
-            hi, lo = split(v.reshape(16, 128))
-            rows = pl.ds(pl.multiple_of(kj * 128 + i * 16, 16), 16)
-            xs_ref[rows, 0:128] = hi
-            xs_ref[rows, 128:256] = lo
-        return 0
-
-    lax.fori_loop(0, 8, fwd, 0)
+def middle(p, r_ref, rs_ref, h_ref, w1_ref, w2_ref, tws_ref, twb_ref, xs_ref, gt_ref, g_ref, sg):
+    for low_k0 in range(2):
+
+        def fwd(i, _):
+            m = low_k0 * 4 + i
+            x = [
+                decode(r_ref[j, p * 8 + m]).reshape(2, 8, 128) * rs_ref[j, p, low_k0 : low_k0 + 1] for j in range(8)
+            ]
+            y = dft8(x, sg)
+            for kj in range(8):
+                v = y[kj]
+                if kj:
+                    v = cmul(v, tws_ref[0, pl.ds(kj, 1)], tws_ref[1, pl.ds(kj, 1)], sg)
+                hi, lo = split(v.reshape(16, 128))
+                rows = pl.ds(pl.multiple_of(kj * 128 + m * 16, 16), 16)
+                xs_ref[rows, 0:128] = hi
+                xs_ref[rows, 128:256] = lo
+            return 0
+
+        lax.fori_loop(0, 4, fwd, 0, unroll=4)
+
+    rows = 512
 
     def dot128(at, sign):
         x = xs_ref[at, :]
         pq = jnp.dot(x, w1_ref[...], preferred_element_type=F32)
         pq = pq + jnp.dot(x[:, 0:128], w2_ref[...], preferred_element_type=F32)
-        return pq[:, 0:128].reshape(16, 8, 128) + swap(pq[:, 128:256].reshape(16, 8, 128)) * sign
+        return pq[:, 0:128].reshape(rows // 8, 8, 128) + swap(pq[:, 128:256].reshape(rows // 8, 8, 128)) * sign
 
     low = lax.broadcasted_iota(jnp.int32, (8, 128), 0) < 4
 
-    def mid(kj, _):
-        at = pl.ds(pl.multiple_of(kj * 128, 128), 128)
+    def mid(i, _):
+        at = pl.ds(pl.multiple_of(i * rows, rows), rows)
         v = dot128(at, sg)
-        h = h_ref[pl.ds(p * 128 + kj * 16, 16)]
+        h = h_ref[pl.ds(p * 128 + i * (rows // 8), rows // 8)]
         hs = swap(h)
         v = v * jnp.where(low, h, hs) + swap(v) * jnp.where(low, -hs, h)
-        hi, lo = split(v.reshape(128, 128))
+        hi, lo = split(v.reshape(rows, 128))
         xs_ref[at, 0:128] = hi
         xs_ref[at, 128:256] = lo
         return 0
 
-    lax.fori_loop(0, 8, mid, 0)
-
-    def back(kj, _):
-        gt_ref[kj] = dot128(pl.ds(pl.multiple_of(kj * 128, 128), 128), -sg)
-        return 0
-
-    lax.fori_loop(0, 8, back, 0)
+    lax.fori_loop(0, 1024 // rows, mid, 0)
+
+    def back(i, _):
+        v = dot128(pl.ds(pl.multiple_of(i * rows, rows), rows), -sg)
+        gt_ref[pl.ds(i * (rows // 128), rows // 128)] = v.reshape(rows // 128, 16, 8, 128)
+        return 0
+
+    lax.fori_loop(0, 1024 // rows, back, 0)
 
     def inv8(i, _):
         at = pl.ds(i * 2, 2)
@@ -294,15 +317,15 @@
             g_ref[here, j] = cmul(y[j], twb_ref[0, here, pl.ds(j, 1)], twb_ref[1, here, pl.ds(j, 1)], -sg)
         return 0
 
-    lax.fori_loop(0, 8, inv8, 0)
+    lax.fori_loop(0, 8, inv8, 0, unroll=4)
 
 
 def kernel(
     d_ref, dm_ref, x_hbm, bw_ref, w1_hbm, w2_hbm, tws_hbm, twb_hbm, twi_hbm,
-    recv3,
+    recv3, rscale3,
     x_ref, w1_ref, w2_ref, tws_ref, twb_ref, twi_ref,
-    xf_ref, send1, recv1, w_ref, bm_ref, send2, recv2, base_ref, h_ref, xs_ref, gt_ref, g_ref, send3,
-    load_sem, sem1, rsem1, sem2, rsem2, sem3, rsem3,
+    xf_ref, send1, recv1, w_ref, bm_ref, send2, scale2, recv2, rscale2, base_ref, h_ref, xs_ref, gt_ref, g_ref, send3, scale3,
+    load_sem, col_sem, sem1, rsem1, sem2, rsem2, ssem2, rssem2, sem3, rsem3, ssem3, rssem3,
 ):
     sub, sta = lax.axis_index("sub"), lax.axis_index("sta")
     me = sub * STA + sta
@@ -320,12 +343,10 @@
 
     barrier = pltpu.get_barrier_semaphore()
 
-    def greet(i, _):
-        d = (me + i) % (SUB * STA)
-        pl.semaphore_signal(barrier, inc=1, device_id={"sub": d // STA, "sta": d % STA}, device_id_type=MESH)
-        return 0
-
-    lax.fori_loop(1, SUB * STA, greet, 0)
+    for i in range(1, STA):
+        pl.semaphore_signal(barrier, inc=1, device_id={"sub": sub, "sta": (sta + i) % STA}, device_id_type=MESH)
+    for i in range(1, SUB):
+        pl.semaphore_signal(barrier, inc=1, device_id={"sub": (sub + i) % SUB, "sta": sta}, device_id_type=MESH)
     x_load.wait()
     unpack_voltages(x_ref, xf_ref)
     setup = delay_setup(d_ref)
@@ -334,7 +355,11 @@
         delay_rows(setup, xf_ref, send1, 2 * part)
         delay_rows(setup, xf_ref, send1, 2 * part + 1)
         if part == 0:
-            pl.semaphore_wait(barrier, SUB * STA - 1)
+            pl.semaphore_wait(barrier, SUB + STA - 2)
+            for i in range(1, STA):
+                pl.semaphore_signal(
+                    col_sem, inc=1, device_id={"sub": sub, "sta": (sta + i) % STA}, device_id_type=MESH
+                )
         cols = pl.ds(part * 2048, 2048)
 
         def go1(i, _):
@@ -366,23 +391,19 @@
         inner_pass(bm_ref, 2 * part + 1, twi_ref, sg)
 
     for part in range(CH):
-
-        def step(low, _):
-            k0 = 2 * part + low
-
-            def put(k1, g, v):
-                k = 8 * k0 + k1
-                v = cmul(v, twb_ref[0, k, pl.ds(sta, 1)], twb_ref[1, k, pl.ds(sta, 1)], sg)
-                send2[pl.ds(2 * g, 2), k] = v
-
-            outer_pass(bm_ref, k0, sg, put)
-            return 0
-
-        lax.fori_loop(0, 2, step, 0)
-        rows = pl.ds(part * 16, 16)
+        outer_and_encode(bm_ref, part, sta, twb_ref, sg, send2, scale2)
+        rows = pl.ds(part * 8, 8)
 
         def go2(i, _):
             d = (sta + i) % STA
+            pltpu.make_async_remote_copy(
+                src_ref=scale2.at[d, part],
+                dst_ref=rscale2.at[sta, part],
+                send_sem=ssem2,
+                recv_sem=rssem2.at[part],
+                device_id={"sub": sub, "sta": d},
+                device_id_type=MESH,
+            ).start()
             pltpu.make_async_remote_copy(
                 src_ref=send2.at[d, rows],
                 dst_ref=recv2.at[sta, rows],
@@ -394,27 +415,42 @@
             return 0
 
         lax.fori_loop(1, STA, go2, 0)
+        pltpu.make_async_copy(scale2.at[sta, part], rscale2.at[sta, part], rssem2.at[part]).start()
         pltpu.make_async_copy(send2.at[sta, rows], recv2.at[sta, rows], rsem2.at[part]).start()
 
     for part in range(CH):
-        rows = pl.ds(part * 16, 16)
+        rows = pl.ds(part * 8, 8)
+        pltpu.make_async_copy(rscale2.at[:, part], rscale2.at[:, part], rssem2.at[part]).wait()
         pltpu.make_async_copy(recv2.at[:, rows], recv2.at[:, rows], rsem2.at[part]).wait()
-        middle(part, recv2, h_ref, w1_ref, w2_ref, tws_ref, twb_ref, xs_ref, gt_ref, g_ref, sg)
+        middle(part, recv2, rscale2, h_ref, w1_ref, w2_ref, tws_ref, twb_ref, xs_ref, gt_ref, g_ref, sg)
         inner_pass(g_ref, 2 * part, twi_ref, -sg)
         inner_pass(g_ref, 2 * part + 1, twi_ref, -sg)
 
+    pl.semaphore_wait(col_sem, STA - 1)
+
     def group(i, _):
         a0 = (sta + i) % 8
-        for g in range(4):
-            y = dft8([g_ref[8 * k0 + a0, pl.ds(2 * g, 2)] for k0 in range(8)], -sg)
+        for jh in range(2):
+            y = dft8([g_ref[8 * k0 + a0, pl.ds(4 * jh, 4)] for k0 in range(8)], -sg)
             for a1 in range(8):
-                send3[2 * (8 * a1 + a0) + g // 2, pl.ds(2 * (g % 2), 2)] = y[a1] * (1.0 / N)
+                d = 16 * a1 + 2 * a0 + jh
+                q, scale = encode(y[a1], (0, 1))
+                send3[d] = q.reshape(2, 16, 128).astype(jnp.int16)
+                scale3[d] = scale.reshape(1, 128) * (1.0 / N)
 
         def go3(n, _):
             d = (16 * (n // 2 + sub // 2) + 2 * a0 + n % 2) % (SUB * STA)
 
             @pl.when(d != me)
             def _():
+                pltpu.make_async_remote_copy(
+                    src_ref=scale3.at[d],
+                    dst_ref=rscale3.at[me],
+                    send_sem=ssem3,
+                    recv_sem=rssem3.at[sub],
+                    device_id={"sub": d // STA, "sta": d % STA},
+                    device_id_type=MESH,
+                ).start()
                 pltpu.make_async_remote_copy(
                     src_ref=send3.at[d],
                     dst_ref=recv3.at[me],
@@ -426,6 +462,7 @@
 
             @pl.when(d == me)
             def _():
+                pltpu.make_async_copy(scale3.at[me], rscale3.at[me], rssem3.at[sub]).start()
                 pltpu.make_async_copy(send3.at[me], recv3.at[me], rsem3.at[sub]).start()
 
             return 0
@@ -438,29 +475,48 @@
     for s in range(SUB):
         block = recv3.at[pl.ds(s * STA, STA)]
         pltpu.make_async_copy(block, block, rsem3.at[s]).wait()
+        block = rscale3.at[pl.ds(s * STA, STA)]
+        pltpu.make_async_copy(block, block, rssem3.at[s]).wait()
     others = pl.ds(0, STA - 1)
     pltpu.make_async_copy(send1.at[others], send1.at[others], sem1).wait()
     pltpu.make_async_copy(send2.at[others], send2.at[others], sem2).wait()
+    pltpu.make_async_copy(scale2.at[others], scale2.at[others], ssem2).wait()
     others = pl.ds(0, SUB * STA - 1)
     pltpu.make_async_copy(send3.at[others], send3.at[others], sem3).wait()
-
-
-def assemble(r_ref, out_ref, int_ref):
-    s = pl.program_id(0)
-
-    @pl.when(s == 0)
-    def _():
-        int_ref[...] = jnp.zeros_like(int_ref)
-
+    pltpu.make_async_copy(scale3.at[others], scale3.at[others], ssem3).wait()
+
+
+def assemble(q_hbm, s_ref, out_hbm, int_ref, q_ref, out_ref, acc_ref, in_sem, out_sem):
+    step = 4 * STA
+    loads = []
+    for i in range(4):
+        part = pl.ds(i * step, step)
+        loads.append(pltpu.make_async_copy(q_hbm.at[part], q_ref.at[part], in_sem.at[i]))
+        loads[-1].start()
+    acc_ref[...] = jnp.zeros_like(acc_ref)
+
+    def one(s, _):
+        for sta in range(STA):
+            src = s * STA + sta
+            v = decode(q_ref[src].reshape(32, 128)).reshape(4, 8, 128) * s_ref[src]
+            acc_ref[sta] += v * v
+            for j4 in range(4):
+                for ri in range(2):
+                    first = s * 256 + (ri * 128 + sta * 16 + j4)
+                    out_ref[pl.ds(first, 4, stride=4), :] = v[j4, 4 * ri : 4 * ri + 4]
+        rows = pl.ds(pl.multiple_of(s * 256, 256), 256)
+        pltpu.make_async_copy(out_ref.at[rows], out_hbm.at[rows], out_sem).start()
+        return 0
+
+    for i in range(4):
+        loads[i].wait()
+        lax.fori_loop(4 * i, 4 * i + 4, one, 0)
     for sta in range(STA):
-        parts = []
-        for ri in range(2):
-            rows = [r_ref[pl.ds(sta * 32 + ri * 4 + b4, 4, stride=8), :] for b4 in range(4)]
-            block = jnp.concatenate(rows, axis=0)
-            out_ref[pl.ds(ri * 128 + sta * 16, 16), :] = block
-            parts.append(block)
-        at = pl.ds(sta * 16, 16)
-        int_ref[at, :] += (parts[0] * parts[0] + parts[1] * parts[1]) * (1.0 / SUB)
+        for j4 in range(4):
+            v = acc_ref[sta, j4]
+            v = (v + swap(v)) * (1.0 / SUB)
+            int_ref[pl.ds(sta * 16 + j4, 4, stride=4), :] = v[0:4]
+    pltpu.make_async_copy(out_ref, out_hbm, out_sem).wait()
 
 
 VM = pl.BlockSpec(memory_space=pltpu.VMEM)
@@ -471,11 +527,14 @@
 def shards(voltages, beam_weights, station_delays, dm_index):
     w1, w2 = dft_tables()
     big, small, inner = twist_tables()
-    moved = pl.pallas_call(
+    moved, scales = pl.pallas_call(
         kernel,
-        out_shape=jax.ShapeDtypeStruct((128, 4, 8, 128), F32),
+        out_shape=(
+            jax.ShapeDtypeStruct((128, 2, 16, 128), jnp.int16),
+            jax.ShapeDtypeStruct((128, 1, 128), F32),
+        ),
         in_specs=[SM, SM, ANY, VM, ANY, ANY, ANY, ANY, ANY],
-        out_specs=ANY,
+        out_specs=(ANY, ANY),
         scratch_shapes=[
             pltpu.VMEM((1, 2, 8, N), BF16),
             pltpu.VMEM((256, 256), BF16),
@@ -488,19 +547,27 @@
             pltpu.VMEM((8, 16, 8192), BF16),
             pltpu.VMEM((64, 128), BF16),
             pltpu.VMEM((64, 8, 8, 128), F32),
-            pltpu.VMEM((8, 64, 8, 128), F32),
-            pltpu.VMEM((8, 64, 8, 128), F32),
+            pltpu.VMEM((8, 32, 16, 128), jnp.int16),
+            pltpu.VMEM((8, CH, 2, 128), F32),
+            pltpu.VMEM((8, 32, 16, 128), jnp.int16),
+            pltpu.VMEM((8, CH, 2, 128), F32),
             pltpu.VMEM((512, 128), F32),
             pltpu.VMEM((512, 8, 128), F32),
             pltpu.VMEM((1024, 256), BF16),
             pltpu.VMEM((8, 16, 8, 128), F32),
             pltpu.VMEM((64, 8, 8, 128), F32),
-            pltpu.VMEM((128, 4, 8, 128), F32),
+            pltpu.VMEM((128, 2, 16, 128), jnp.int16),
+            pltpu.VMEM((128, 1, 128), F32),
             pltpu.SemaphoreType.DMA((6,)),
+            pltpu.SemaphoreType.REGULAR,
             pltpu.SemaphoreType.DMA,
             pltpu.SemaphoreType.DMA((CH,)),
             pltpu.SemaphoreType.DMA,
             pltpu.SemaphoreType.DMA((CH,)),
+            pltpu.SemaphoreType.DMA,
+            pltpu.SemaphoreType.DMA((CH,)),
+            pltpu.SemaphoreType.DMA,
+            pltpu.SemaphoreType.DMA((SUB,)),
             pltpu.SemaphoreType.DMA,
             pltpu.SemaphoreType.DMA((SUB,)),
         ],
@@ -508,17 +575,22 @@
             collective_id=0, has_side_effects=True, vmem_limit_bytes=60 * 1024 * 1024
         ),
     )(
-        station_delays, dm_index, voltages, beam_weights,
+        station_delays, dm_index.reshape(4), voltages, beam_weights,
         jnp.asarray(w1), jnp.asarray(w2), jnp.asarray(small), jnp.asarray(big), jnp.asarray(inner),
     )
     out, power = pl.pallas_call(
         assemble,
-        grid=(SUB,),
         out_shape=(jax.ShapeDtypeStruct((4096, 128), F32), jax.ShapeDtypeStruct((128, 128), F32)),
-        in_specs=[pl.BlockSpec((256, 128), lambda s: (s, 0))],
-        out_specs=(pl.BlockSpec((256, 128), lambda s: (s, 0)), pl.BlockSpec((128, 128), lambda s: (0, 0))),
-        compiler_params=pltpu.CompilerParams(dimension_semantics=("arbitrary",)),
-    )(moved.reshape(4096, 128))
+        in_specs=[ANY, VM],
+        out_specs=(ANY, VM),
+        scratch_shapes=[
+            pltpu.VMEM((128, 2, 16, 128), jnp.int16),
+            pltpu.VMEM((4096, 128), F32),
+            pltpu.VMEM((STA, 4, 8, 128), F32),
+            pltpu.SemaphoreType.DMA((4,)),
+            pltpu.SemaphoreType.DMA,
+        ],
+    )(moved, scales)
     return out.reshape(16, 2, 32, 1, 512), power.reshape(32, 1, 512)
 
 

time: 106 us -> 72.8 us (0.69)
  Pallas kernels: 103 us -> 71.7 us
  local copies, waits for them, and re-layouts: 1.31 us -> 0 us
    pallas_call x2, Pallas kernels: 103 us -> 71.7 us  [the longest x1 67.9 us: shards(): pl.pallas_call(kernel, out_shape=(jax.ShapeDtypeStruct((128, 2, 16, 128),...]
    unnamed x1 -> x0, local copies, waits for them, and re-layouts: 1.31 us -> none
where the time goes in v3:
time: 72.8 us; the launch traced here: 72.3 us
  Pallas kernels  71.7 us (98%)
    pallas_call x1, Pallas kernels, shards(): pl.pallas_call(kernel, out_shape=(jax.ShapeDtypeStruct((128, 2, 16, 128),...  67.9 us
    pallas_call x1, Pallas kernels, shards(): pl.pallas_call(assemble, out_shape=(jax.ShapeDtypeStruct((4096, 128), F32...  3.78 us

profile of v3, /device:TPU:0, one launch (start us, length us, event | category | flops | bytes accessed | tf_op | source)
XLA Modules:
  0.0 72.3 jit_solution(5809731188793587659)
XLA Ops:
  0.6 67.9 %shard_map.104 = (s16[128,2,16,128]{3,2,1,0:T(8,128)(2,1)}, f32[128,1,128]{2,1,0:T(1,128)}) custom-call(s32[8]{0:T(128)} %d_ref.1, s32[4]{0:T(128)} %bitcast.3, bf16[1,2,8,65536]{3,2,1,0:T(8,128)(2,1)} %x_hbm.1, bf16[1,2,32,64]{3,2,1,0:T(8,128)(2,1)} %bw_ref.1, bf16[256,256]{1,0:T(8,128)(2,1)} %constant.10.clone.w1_hbm, ...), custom_call_target="tpu_custom_call" | custom-call | tf_op jit(solution)/shard_map/pallas_call | solution.py:530
  68.5 3.8 %shard_map.105 = (f32[4096,128]{1,0:T(8,128)}, f32[128,128]{1,0:T(8,128)}) custom-call(s16[128,2,16,128]{3,2,1,0:T(8,128)(2,1)} %get-tuple-element.6.q_hbm, f32[128,1,128]{2,1,0:T(1,128)} %get-tuple-element.7.s_ref), custom_call_target="tpu_custom_call" | custom-call | tf_op jit(solution)/shard_map/pallas_call | solution.py:581

commit v4 on v3

--- a/solution.py
+++ b/solution.py
@@ -23,7 +23,8 @@
 
 MESH = pl.DeviceIdType.MESH
 TOP = 32767.0
-CH = 4
+CH = 8
+LOADS = 4
 
 
 def dft_tables():
@@ -85,23 +86,27 @@
     return hi, lo
 
 
-def unpack_voltages(x_ref, xf_ref):
+def unpack_voltages(x_ref, xf_ref, piece):
+    per = 512 // LOADS
+
     def body(i, _):
         for u in range(8):
-            t = i * 8 + u
+            t = piece * per + i * 8 + u
             col = pl.multiple_of(t * 128, 128)
             for ri in range(2):
                 xf_ref[ri, t + 128] = x_ref[0, ri, :, pl.ds(col, 128)].astype(F32)
         return 0
 
-    lax.fori_loop(0, 64, body, 0)
-
+    lax.fori_loop(0, per // 8, body, 0)
+
+
+def wrap_voltages(xf_ref):
     def wrap(i, _):
         for ri in range(2):
             xf_ref[ri, pl.ds(i * 8, 8)] = xf_ref[ri, pl.ds(i * 8 + 512, 8)]
         return 0
 
-    lax.fori_loop(0, 16, wrap, 0)
+    lax.fori_loop(0, 16, wrap, 0, unroll=4)
 
 
 def delay_setup(d_ref):
@@ -133,7 +138,7 @@
             out_ref[j, :, pl.ds(col, 128)] = jnp.concatenate([done[0][j], done[1][j]], axis=0).astype(BF16)
         return 0
 
-    lax.fori_loop(0, 8, body, 0)
+    lax.fori_loop(0, 8, body, 0, unroll=2)
 
 
 def one_hot(shape, hit):
@@ -158,14 +163,14 @@
     w = w_ref[...]
 
     def body(i, _):
-        first = part * 16 + i * 4
+        first = part * 8 + i * 4
         v = v_ref[:, :, pl.ds(pl.multiple_of(first * 128, 512), 512)].reshape(128, 512)
         out = jnp.dot(w, v, preferred_element_type=F32)
         for u in range(4):
             bm_ref[first + u] = out[:, u * 128 : (u + 1) * 128].reshape(8, 8, 128)
         return 0
 
-    lax.fori_loop(0, 4, body, 0)
+    lax.fori_loop(0, 2, body, 0, unroll=2)
 
 
 def inner_pass(ref, lead, twi_ref, sg):
@@ -192,19 +197,17 @@
     return ints.astype(jnp.int32).astype(F32)
 
 
-def outer_and_encode(bm_ref, part, sta, twb_ref, sg, q_ref, s_ref):
-    for low in range(2):
-        k0 = 2 * part + low
-        for g in range(4):
-            at = pl.ds(2 * g, 2)
-            y = dft8([bm_ref[8 * i + k0, at] for i in range(8)], sg)
-            out = []
-            for k1 in range(8):
-                k = 8 * k0 + k1
-                out.append(cmul(y[k1], twb_ref[0, k, pl.ds(sta, 1)], twb_ref[1, k, pl.ds(sta, 1)], sg))
-            q, scale = encode(jnp.stack(out, axis=1), (1, 2))
-            q_ref[at, pl.ds(4 * k0, 4)] = q.reshape(2, 4, 16, 128).astype(jnp.int16)
-            s_ref[at, part, low : low + 1] = scale.reshape(2, 1, 128)
+def outer_and_encode(bm_ref, k0, sta, twb_ref, sg, q_ref, s_ref):
+    for g in range(4):
+        at = pl.ds(2 * g, 2)
+        y = dft8([bm_ref[8 * i + k0, at] for i in range(8)], sg)
+        out = []
+        for k1 in range(8):
+            k = 8 * k0 + k1
+            out.append(cmul(y[k1], twb_ref[0, k, pl.ds(sta, 1)], twb_ref[1, k, pl.ds(sta, 1)], sg))
+        q, scale = encode(jnp.stack(out, axis=1), (1, 2))
+        q_ref[at, pl.ds(4 * k0, 4)] = q.reshape(2, 4, 16, 128).astype(jnp.int16)
+        s_ref[at, k0] = scale.reshape(2, 1, 128)
 
 
 def chirp_table(dm_ref, base_ref, h_ref):
@@ -215,8 +218,8 @@
     )
 
     def base(i, _):
-        part, kj, low = i // 16, (i // 2) % 8, i % 2
-        positions = 8 * row + (2 * part + low) + 64 * kj + 512 * lane
+        k0, kj = i // 8, i % 8
+        positions = 8 * row + k0 + 64 * kj + 512 * lane
         signed_bin = jnp.where(positions < N // 2, positions, positions - N)
         offset = CHANNEL_WIDTH * signed_bin.astype(F32) / N
         base_ref[pl.ds(pl.multiple_of(i * 8, 8), 8), :] = (
@@ -252,117 +255,93 @@
     lax.fori_loop(0, 128, body, 0)
 
 
-def middle(p, r_ref, rs_ref, h_ref, w1_ref, w2_ref, tws_ref, twb_ref, xs_ref, gt_ref, g_ref, sg):
-    for low_k0 in range(2):
-
-        def fwd(i, _):
-            m = low_k0 * 4 + i
-            x = [
-                decode(r_ref[j, p * 8 + m]).reshape(2, 8, 128) * rs_ref[j, p, low_k0 : low_k0 + 1] for j in range(8)
-            ]
-            y = dft8(x, sg)
-            for kj in range(8):
-                v = y[kj]
-                if kj:
-                    v = cmul(v, tws_ref[0, pl.ds(kj, 1)], tws_ref[1, pl.ds(kj, 1)], sg)
-                hi, lo = split(v.reshape(16, 128))
-                rows = pl.ds(pl.multiple_of(kj * 128 + m * 16, 16), 16)
-                xs_ref[rows, 0:128] = hi
-                xs_ref[rows, 128:256] = lo
-            return 0
-
-        lax.fori_loop(0, 4, fwd, 0, unroll=4)
-
-    rows = 512
-
-    def dot128(at, sign):
-        x = xs_ref[at, :]
+def middle(k0, r_ref, rs_ref, h_ref, w1_ref, w2_ref, tws_ref, twb_ref, xs_ref, gt_ref, g_ref, sg):
+    for m in range(4):
+        x = [decode(r_ref[j, k0 * 4 + m]).reshape(2, 8, 128) * rs_ref[j, k0] for j in range(8)]
+        y = dft8(x, sg)
+        for kj in range(8):
+            v = y[kj]
+            if kj:
+                v = cmul(v, tws_ref[0, pl.ds(kj, 1)], tws_ref[1, pl.ds(kj, 1)], sg)
+            hi, lo = split(v.reshape(16, 128))
+            at = kj * 64 + m * 16
+            xs_ref[at : at + 16, 0:128] = hi
+            xs_ref[at : at + 16, 128:256] = lo
+
+    def dot128(sign):
+        x = xs_ref[...]
         pq = jnp.dot(x, w1_ref[...], preferred_element_type=F32)
         pq = pq + jnp.dot(x[:, 0:128], w2_ref[...], preferred_element_type=F32)
-        return pq[:, 0:128].reshape(rows // 8, 8, 128) + swap(pq[:, 128:256].reshape(rows // 8, 8, 128)) * sign
+        return pq[:, 0:128].reshape(64, 8, 128) + swap(pq[:, 128:256].reshape(64, 8, 128)) * sign
 
     low = lax.broadcasted_iota(jnp.int32, (8, 128), 0) < 4
-
-    def mid(i, _):
-        at = pl.ds(pl.multiple_of(i * rows, rows), rows)
-        v = dot128(at, sg)
-        h = h_ref[pl.ds(p * 128 + i * (rows // 8), rows // 8)]
-        hs = swap(h)
-        v = v * jnp.where(low, h, hs) + swap(v) * jnp.where(low, -hs, h)
-        hi, lo = split(v.reshape(rows, 128))
-        xs_ref[at, 0:128] = hi
-        xs_ref[at, 128:256] = lo
-        return 0
-
-    lax.fori_loop(0, 1024 // rows, mid, 0)
-
-    def back(i, _):
-        v = dot128(pl.ds(pl.multiple_of(i * rows, rows), rows), -sg)
-        gt_ref[pl.ds(i * (rows // 128), rows // 128)] = v.reshape(rows // 128, 16, 8, 128)
-        return 0
-
-    lax.fori_loop(0, 1024 // rows, back, 0)
-
-    def inv8(i, _):
-        at = pl.ds(i * 2, 2)
+    v = dot128(sg)
+    h = h_ref[pl.ds(k0 * 64, 64)]
+    hs = swap(h)
+    v = v * jnp.where(low, h, hs) + swap(v) * jnp.where(low, -hs, h)
+    hi, lo = split(v.reshape(512, 128))
+    xs_ref[:, 0:128] = hi
+    xs_ref[:, 128:256] = lo
+    gt_ref[...] = dot128(-sg).reshape(8, 8, 8, 128)
+
+    for i in range(4):
         x = []
         for kj in range(8):
-            v = gt_ref[kj, at]
+            v = gt_ref[kj, 2 * i : 2 * i + 2]
             if kj:
                 v = cmul(v, tws_ref[0, pl.ds(kj, 1)], tws_ref[1, pl.ds(kj, 1)], -sg)
             x.append(v)
         y = dft8(x, -sg)
-        here = pl.ds(p * 16 + i * 2, 2)
+        here = pl.ds(k0 * 8 + i * 2, 2)
         for j in range(8):
             g_ref[here, j] = cmul(y[j], twb_ref[0, here, pl.ds(j, 1)], twb_ref[1, here, pl.ds(j, 1)], -sg)
-        return 0
-
-    lax.fori_loop(0, 8, inv8, 0, unroll=4)
+
+
+PLACES = ((0, 2, 1), (1, 0, 0), (0, 1, 0), (1, 3, 1), (0, 0, 1), (1, 2, 0), (0, 3, 0), (1, 1, 1), (0, 2, 0), (1, 0, 1), (0, 1, 1), (1, 3, 0), (0, 3, 1), (1, 1, 0), (1, 2, 1), (0, 0, 0))
 
 
 def kernel(
-    d_ref, dm_ref, x_hbm, bw_ref, w1_hbm, w2_hbm, tws_hbm, twb_hbm, twi_hbm,
+    d_hbm, dm_hbm, x_hbm, bw_hbm, w1_hbm, w2_hbm, tws_hbm, twb_hbm, twi_hbm,
     recv3, rscale3,
-    x_ref, w1_ref, w2_ref, tws_ref, twb_ref, twi_ref,
-    xf_ref, send1, recv1, w_ref, bm_ref, send2, scale2, recv2, rscale2, base_ref, h_ref, xs_ref, gt_ref, g_ref, send3, scale3,
+    d_ref, dm_ref, bw_ref, x_ref, w1_ref, w2_ref, tws_ref, twb_ref, twi_ref,
+    xf_ref, send1, recv1, w_ref, bm_ref, send2, scale2, recv2, rscale2, base_ref, h_ref, xs_ref, gt_ref, g_ref,
+    send3, scale3,
     load_sem, col_sem, sem1, rsem1, sem2, rsem2, ssem2, rssem2, sem3, rsem3, ssem3, rssem3,
 ):
     sub, sta = lax.axis_index("sub"), lax.axis_index("sta")
     me = sub * STA + sta
 
-    x_load = pltpu.make_async_copy(x_hbm, x_ref, load_sem.at[0])
-    x_load.start()
+    x_loads = []
+    for i in range(LOADS):
+        cols = pl.ds(i * (N // LOADS), N // LOADS)
+        x_loads.append(pltpu.make_async_copy(x_hbm.at[:, :, :, cols], x_ref.at[:, :, :, cols], load_sem.at[i]))
     tables = [
-        pltpu.make_async_copy(a, b, load_sem.at[1 + i])
+        pltpu.make_async_copy(a, b, load_sem.at[LOADS + i])
         for i, (a, b) in enumerate(
-            [(w1_hbm, w1_ref), (w2_hbm, w2_ref), (tws_hbm, tws_ref), (twb_hbm, twb_ref), (twi_hbm, twi_ref)]
+            [
+                (d_hbm, d_ref), (dm_hbm, dm_ref), (bw_hbm, bw_ref), (w1_hbm, w1_ref), (w2_hbm, w2_ref),
+                (tws_hbm, tws_ref), (twb_hbm, twb_ref), (twi_hbm, twi_ref),
+            ]
         )
     ]
-    for t in tables:
+    for t in tables[:1] + x_loads + tables[1:]:
         t.start()
 
     barrier = pltpu.get_barrier_semaphore()
-
     for i in range(1, STA):
         pl.semaphore_signal(barrier, inc=1, device_id={"sub": sub, "sta": (sta + i) % STA}, device_id_type=MESH)
     for i in range(1, SUB):
         pl.semaphore_signal(barrier, inc=1, device_id={"sub": (sub + i) % SUB, "sta": sta}, device_id_type=MESH)
-    x_load.wait()
-    unpack_voltages(x_ref, xf_ref)
+    for i in range(LOADS):
+        x_loads[i].wait()
+        unpack_voltages(x_ref, xf_ref, i)
+    wrap_voltages(xf_ref)
+    tables[0].wait()
     setup = delay_setup(d_ref)
 
-    for part in range(CH):
-        delay_rows(setup, xf_ref, send1, 2 * part)
-        delay_rows(setup, xf_ref, send1, 2 * part + 1)
-        if part == 0:
-            pl.semaphore_wait(barrier, SUB + STA - 2)
-            for i in range(1, STA):
-                pl.semaphore_signal(
-                    col_sem, inc=1, device_id={"sub": sub, "sta": (sta + i) % STA}, device_id_type=MESH
-                )
-        cols = pl.ds(part * 2048, 2048)
-
-        def go1(i, _):
+    def first(part):
+        cols = pl.ds(pl.multiple_of(part * 1024, 1024), 1024)
+        for i in range(1, STA):
             d = (sta + i) % STA
             pltpu.make_async_remote_copy(
                 src_ref=send1.at[d, :, cols],
@@ -372,29 +351,40 @@
                 device_id={"sub": sub, "sta": d},
                 device_id_type=MESH,
             ).start()
-            return 0
-
-        lax.fori_loop(1, STA, go1, 0)
         pltpu.make_async_copy(send1.at[sta, :, cols], recv1.at[sta, :, cols], rsem1.at[part]).start()
 
+    delay_rows(setup, xf_ref, send1, 0)
+    pl.semaphore_wait(barrier, SUB + STA - 2)
+    first(0)
+    for i in range(1, STA):
+        pl.semaphore_signal(col_sem, inc=1, device_id={"sub": sub, "sta": (sta + i) % STA}, device_id_type=MESH)
+
+    def more(part, _):
+        delay_rows(setup, xf_ref, send1, part)
+        first(part)
+        return 0
+
+    lax.fori_loop(1, CH, more, 0)
+
+    for t in tables[1:]:
+        t.wait()
     w_ref[...] = stacked_weights(bw_ref)
     chirp_table(dm_ref, base_ref, h_ref)
-    for t in tables:
-        t.wait()
     sg = sign_rows()
 
-    for part in range(CH):
-        cols = pl.ds(part * 2048, 2048)
+    def beams(part, _):
+        cols = pl.ds(pl.multiple_of(part * 1024, 1024), 1024)
         pltpu.make_async_copy(recv1.at[:, :, cols], recv1.at[:, :, cols], rsem1.at[part]).wait()
         beamform(w_ref, recv1, bm_ref, part)
-        inner_pass(bm_ref, 2 * part, twi_ref, sg)
-        inner_pass(bm_ref, 2 * part + 1, twi_ref, sg)
-
-    for part in range(CH):
+        inner_pass(bm_ref, part, twi_ref, sg)
+        return 0
+
+    lax.fori_loop(0, CH, beams, 0)
+
+    def second(part, _):
         outer_and_encode(bm_ref, part, sta, twb_ref, sg, send2, scale2)
-        rows = pl.ds(part * 8, 8)
-
-        def go2(i, _):
+        rows = pl.ds(part * 4, 4)
+        for i in range(1, STA):
             d = (sta + i) % STA
             pltpu.make_async_remote_copy(
                 src_ref=scale2.at[d, part],
@@ -412,24 +402,28 @@
                 device_id={"sub": sub, "sta": d},
                 device_id_type=MESH,
             ).start()
-            return 0
-
-        lax.fori_loop(1, STA, go2, 0)
         pltpu.make_async_copy(scale2.at[sta, part], rscale2.at[sta, part], rssem2.at[part]).start()
         pltpu.make_async_copy(send2.at[sta, rows], recv2.at[sta, rows], rsem2.at[part]).start()
-
-    for part in range(CH):
-        rows = pl.ds(part * 8, 8)
+        return 0
+
+    lax.fori_loop(0, CH, second, 0)
+
+    def spectra(part, _):
+        rows = pl.ds(part * 4, 4)
         pltpu.make_async_copy(rscale2.at[:, part], rscale2.at[:, part], rssem2.at[part]).wait()
         pltpu.make_async_copy(recv2.at[:, rows], recv2.at[:, rows], rsem2.at[part]).wait()
         middle(part, recv2, rscale2, h_ref, w1_ref, w2_ref, tws_ref, twb_ref, xs_ref, gt_ref, g_ref, sg)
-        inner_pass(g_ref, 2 * part, twi_ref, -sg)
-        inner_pass(g_ref, 2 * part + 1, twi_ref, -sg)
+        inner_pass(g_ref, part, twi_ref, -sg)
+        return 0
+
+    lax.fori_loop(0, CH, spectra, 0)
 
     pl.semaphore_wait(col_sem, STA - 1)
+    x_hi, z, core = sub // 8, (sub // 2) % 4, sub % 2
+    x_lo, yh, jh_own = sta // 4, (sta // 2) % 2, sta % 2
 
     def group(i, _):
-        a0 = (sta + i) % 8
+        a0 = 4 * ((core + 1 - (i // 4) % 2) % 2) + 2 * ((x_lo + 1 - (i // 2) % 2) % 2) + (yh + 1 - i % 2) % 2
         for jh in range(2):
             y = dft8([g_ref[8 * k0 + a0, pl.ds(4 * jh, 4)] for k0 in range(8)], -sg)
             for a1 in range(8):
@@ -438,11 +432,10 @@
                 send3[d] = q.reshape(2, 16, 128).astype(jnp.int16)
                 scale3[d] = scale.reshape(1, 128) * (1.0 / N)
 
-        def go3(n, _):
-            d = (16 * (n // 2 + sub // 2) + 2 * a0 + n % 2) % (SUB * STA)
-
-            @pl.when(d != me)
-            def _():
+        for dx, dz, dj in PLACES:
+            d = 64 * ((x_hi + dx) % 2) + 16 * ((z + dz) % 4) + 2 * a0 + (jh_own + dj) % 2
+
+            def go():
                 pltpu.make_async_remote_copy(
                     src_ref=scale3.at[d],
                     dst_ref=rscale3.at[me],
@@ -460,14 +453,16 @@
                     device_id_type=MESH,
                 ).start()
 
-            @pl.when(d == me)
-            def _():
-                pltpu.make_async_copy(scale3.at[me], rscale3.at[me], rssem3.at[sub]).start()
-                pltpu.make_async_copy(send3.at[me], recv3.at[me], rsem3.at[sub]).start()
-
-            return 0
-
-        lax.fori_loop(0, 16, go3, 0)
+            if dx or dz or dj:
+                go()
+            else:
+                pl.when(d != me)(go)
+
+                @pl.when(d == me)
+                def _():
+                    pltpu.make_async_copy(scale3.at[me], rscale3.at[me], rssem3.at[sub]).start()
+                    pltpu.make_async_copy(send3.at[me], recv3.at[me], rsem3.at[sub]).start()
+
         return 0
 
     lax.fori_loop(0, 8, group, 0)
@@ -486,13 +481,7 @@
     pltpu.make_async_copy(scale3.at[others], scale3.at[others], ssem3).wait()
 
 
-def assemble(q_hbm, s_ref, out_hbm, int_ref, q_ref, out_ref, acc_ref, in_sem, out_sem):
-    step = 4 * STA
-    loads = []
-    for i in range(4):
-        part = pl.ds(i * step, step)
-        loads.append(pltpu.make_async_copy(q_hbm.at[part], q_ref.at[part], in_sem.at[i]))
-        loads[-1].start()
+def assemble(q_ref, s_ref, out_hbm, int_ref, out_ref, acc_ref, out_sem):
     acc_ref[...] = jnp.zeros_like(acc_ref)
 
     def one(s, _):
@@ -508,9 +497,7 @@
         pltpu.make_async_copy(out_ref.at[rows], out_hbm.at[rows], out_sem).start()
         return 0
 
-    for i in range(4):
-        loads[i].wait()
-        lax.fori_loop(4 * i, 4 * i + 4, one, 0)
+    lax.fori_loop(0, SUB, one, 0)
     for sta in range(STA):
         for j4 in range(4):
             v = acc_ref[sta, j4]
@@ -522,6 +509,7 @@
 VM = pl.BlockSpec(memory_space=pltpu.VMEM)
 SM = pl.BlockSpec(memory_space=pltpu.SMEM)
 ANY = pl.BlockSpec(memory_space=pl.ANY)
+HBM = pl.BlockSpec(memory_space=pltpu.HBM)
 
 
 def shards(voltages, beam_weights, station_delays, dm_index):
@@ -530,12 +518,15 @@
     moved, scales = pl.pallas_call(
         kernel,
         out_shape=(
-            jax.ShapeDtypeStruct((128, 2, 16, 128), jnp.int16),
-            jax.ShapeDtypeStruct((128, 1, 128), F32),
+            pltpu.VMEM((128, 2, 16, 128), jnp.int16),
+            pltpu.VMEM((128, 1, 128), F32),
         ),
-        in_specs=[SM, SM, ANY, VM, ANY, ANY, ANY, ANY, ANY],
+        in_specs=[HBM] * 9,
         out_specs=(ANY, ANY),
         scratch_shapes=[
+            pltpu.SMEM((8,), jnp.int32),
+            pltpu.SMEM((4,), jnp.int32),
+            pltpu.VMEM((1, 2, 32, 64), BF16),
             pltpu.VMEM((1, 2, 8, N), BF16),
             pltpu.VMEM((256, 256), BF16),
             pltpu.VMEM((128, 256), BF16),
@@ -548,17 +539,17 @@
             pltpu.VMEM((64, 128), BF16),
             pltpu.VMEM((64, 8, 8, 128), F32),
             pltpu.VMEM((8, 32, 16, 128), jnp.int16),
-            pltpu.VMEM((8, CH, 2, 128), F32),
+            pltpu.VMEM((8, CH, 1, 128), F32),
             pltpu.VMEM((8, 32, 16, 128), jnp.int16),
-            pltpu.VMEM((8, CH, 2, 128), F32),
+            pltpu.VMEM((8, CH, 1, 128), F32),
             pltpu.VMEM((512, 128), F32),
             pltpu.VMEM((512, 8, 128), F32),
-            pltpu.VMEM((1024, 256), BF16),
-            pltpu.VMEM((8, 16, 8, 128), F32),
+            pltpu.VMEM((512, 256), BF16),
+            pltpu.VMEM((8, 8, 8, 128), F32),
             pltpu.VMEM((64, 8, 8, 128), F32),
             pltpu.VMEM((128, 2, 16, 128), jnp.int16),
             pltpu.VMEM((128, 1, 128), F32),
-            pltpu.SemaphoreType.DMA((6,)),
+            pltpu.SemaphoreType.DMA((LOADS + 8,)),
             pltpu.SemaphoreType.REGULAR,
             pltpu.SemaphoreType.DMA,
             pltpu.SemaphoreType.DMA((CH,)),
@@ -572,7 +563,7 @@
             pltpu.SemaphoreType.DMA((SUB,)),
         ],
         compiler_params=pltpu.CompilerParams(
-            collective_id=0, has_side_effects=True, vmem_limit_bytes=60 * 1024 * 1024
+            collective_id=0, has_side_effects=True, vmem_limit_bytes=56 * 1024 * 1024
         ),
     )(
         station_delays, dm_index.reshape(4), voltages, beam_weights,
@@ -581,15 +572,14 @@
     out, power = pl.pallas_call(
         assemble,
         out_shape=(jax.ShapeDtypeStruct((4096, 128), F32), jax.ShapeDtypeStruct((128, 128), F32)),
-        in_specs=[ANY, VM],
+        in_specs=[VM, VM],
         out_specs=(ANY, VM),
         scratch_shapes=[
-            pltpu.VMEM((128, 2, 16, 128), jnp.int16),
             pltpu.VMEM((4096, 128), F32),
             pltpu.VMEM((STA, 4, 8, 128), F32),
-            pltpu.SemaphoreType.DMA((4,)),
             pltpu.SemaphoreType.DMA,
         ],
+        compiler_params=pltpu.CompilerParams(vmem_limit_bytes=16 * 1024 * 1024),
     )(moved, scales)
     return out.reshape(16, 2, 32, 1, 512), power.reshape(32, 1, 512)
 

time: 72.8 us -> 67.7 us (0.930)
  Pallas kernels: 71.7 us -> 66.9 us
    pallas_call x1, Pallas kernels: 67.9 us -> 64.9 us  [shards(): pl.pallas_call(kernel, out_shape=(pltpu.VMEM((128, 2, 16, 128), jnp.int16...]
    pallas_call x1, Pallas kernels: 3.78 us -> 1.97 us  [shards(): pl.pallas_call(assemble, out_shape=(jax.ShapeDtypeStruct((4096, 128), F32...]
where the time goes in v4:
time: 67.7 us; the launch traced here: 67.5 us
  Pallas kernels  66.9 us (99%)
    pallas_call x1, Pallas kernels, shards(): pl.pallas_call(kernel, out_shape=(pltpu.VMEM((128, 2, 16, 128), jnp.int16...  64.9 us
    pallas_call x1, Pallas kernels, shards(): pl.pallas_call(assemble, out_shape=(jax.ShapeDtypeStruct((4096, 128), F32...  1.97 us

profile of v4, /device:TPU:0, one launch (start us, length us, event | category | flops | bytes accessed | tf_op | source)
XLA Modules:
  0.0 67.5 jit_solution(16524950357949564555)
XLA Ops:
  0.6 64.9 %shard_map.104 = (s16[128,2,16,128]{3,2,1,0:T(8,128)(2,1)S(1)}, f32[128,1,128]{2,1,0:T(1,128)S(1)}) custom-call(s32[8]{0:T(128)} %d_hbm.1, s32[4]{0:T(128)} %bitcast.3, bf16[1,2,8,65536]{3,2,1,0:T(8,128)(2,1)} %x_hbm.1, bf16[1,2,32,64]{3,2,1,0:T(8,128)(2,1)} %bw_hbm.1, bf16[256,256]{1,0:T(8,128)(2,1)} %constant.10.clone.w1_hbm, ...), custom_call_target="tpu_custom_call" | custom-call | tf_op jit(solution)/shard_map/pallas_call | solution.py:518
  65.6 2.0 %shard_map.105 = (f32[4096,128]{1,0:T(8,128)}, f32[128,128]{1,0:T(8,128)}) custom-call(s16[128,2,16,128]{3,2,1,0:T(8,128)(2,1)S(1)} %get-tuple-element.6.q_ref, f32[128,1,128]{2,1,0:T(1,128)S(1)} %get-tuple-element.7.s_ref), custom_call_target="tpu_custom_call" | custom-call | tf_op jit(solution)/shard_map/pallas_call | solution.py:572

commit v5 on v4

--- a/solution.py
+++ b/solution.py
@@ -25,6 +25,7 @@
 TOP = 32767.0
 CH = 8
 LOADS = 4
+HEAD_START = 10
 
 
 def dft_tables():
@@ -210,7 +211,7 @@
         s_ref[at, k0] = scale.reshape(2, 1, 128)
 
 
-def chirp_table(dm_ref, base_ref, h_ref):
+def chirp_table(dm_ref, base_ref, h_ref, first, last):
     row = lax.broadcasted_iota(jnp.int32, (8, 128), 0)
     lane = lax.broadcasted_iota(jnp.int32, (8, 128), 1)
     centre = BASE_FREQ + CHANNEL_WIDTH * (
@@ -227,7 +228,7 @@
         )
         return 0
 
-    lax.fori_loop(0, 64, base, 0)
+    lax.fori_loop(first * 4, last * 4, base, 0)
     quarter = jnp.where(row < 4, 1, 0)
     dm = jnp.zeros((8, 128), F32)
     for b in range(4):
@@ -252,7 +253,7 @@
             one(i * 4 + u)
         return 0
 
-    lax.fori_loop(0, 128, body, 0)
+    lax.fori_loop(first * 8, last * 8, body, 0)
 
 
 def middle(k0, r_ref, rs_ref, h_ref, w1_ref, w2_ref, tws_ref, twb_ref, xs_ref, gt_ref, g_ref, sg):
@@ -306,7 +307,7 @@
     d_ref, dm_ref, bw_ref, x_ref, w1_ref, w2_ref, tws_ref, twb_ref, twi_ref,
     xf_ref, send1, recv1, w_ref, bm_ref, send2, scale2, recv2, rscale2, base_ref, h_ref, xs_ref, gt_ref, g_ref,
     send3, scale3,
-    load_sem, col_sem, sem1, rsem1, sem2, rsem2, ssem2, rssem2, sem3, rsem3, ssem3, rssem3,
+    load_sem, answer_sem, col_sem, sem1, rsem1, sem2, rsem2, ssem2, rssem2, sem3, rsem3, ssem3, rssem3,
 ):
     sub, sta = lax.axis_index("sub"), lax.axis_index("sta")
     me = sub * STA + sta
@@ -330,8 +331,17 @@
     barrier = pltpu.get_barrier_semaphore()
     for i in range(1, STA):
         pl.semaphore_signal(barrier, inc=1, device_id={"sub": sub, "sta": (sta + i) % STA}, device_id_type=MESH)
-    for i in range(1, SUB):
-        pl.semaphore_signal(barrier, inc=1, device_id={"sub": (sub + i) % SUB, "sta": sta}, device_id_type=MESH)
+    x_hi, z, core = sub // 8, (sub // 2) % 4, sub % 2
+    rank = 4 * z + 2 * x_hi + core
+
+    def column(r):
+        return {"sub": 8 * ((r // 2) % 2) + 2 * (r // 4) + r % 2, "sta": sta}
+
+    def greet(r, _):
+        pl.semaphore_signal(barrier, inc=1, device_id=column(r), device_id_type=MESH)
+        return 0
+
+    lax.fori_loop(rank + 1, SUB, greet, 0)
     for i in range(LOADS):
         x_loads[i].wait()
         unpack_voltages(x_ref, xf_ref, i)
@@ -353,11 +363,18 @@
             ).start()
         pltpu.make_async_copy(send1.at[sta, :, cols], recv1.at[sta, :, cols], rsem1.at[part]).start()
 
+    tables[1].wait()
+    late = HEAD_START * (1 - (sub % 2))
+    chirp_table(dm_ref, base_ref, h_ref, 0, late)
     delay_rows(setup, xf_ref, send1, 0)
-    pl.semaphore_wait(barrier, SUB + STA - 2)
+    pl.semaphore_wait(barrier, STA - 1 + rank)
     first(0)
-    for i in range(1, STA):
-        pl.semaphore_signal(col_sem, inc=1, device_id={"sub": sub, "sta": (sta + i) % STA}, device_id_type=MESH)
+
+    def answer(r, _):
+        pl.semaphore_signal(answer_sem, inc=1, device_id=column(r), device_id_type=MESH)
+        return 0
+
+    lax.fori_loop(0, rank, answer, 0)
 
     def more(part, _):
         delay_rows(setup, xf_ref, send1, part)
@@ -366,10 +383,16 @@
 
     lax.fori_loop(1, CH, more, 0)
 
-    for t in tables[1:]:
+    for t in tables[2:]:
         t.wait()
     w_ref[...] = stacked_weights(bw_ref)
-    chirp_table(dm_ref, base_ref, h_ref)
+    chirp_table(dm_ref, base_ref, h_ref, late, 16)
+    @pl.when(rank < SUB - 1)
+    def _():
+        pl.semaphore_wait(answer_sem, SUB - 1 - rank)
+
+    for i in range(1, STA):
+        pl.semaphore_signal(col_sem, inc=1, device_id={"sub": sub, "sta": (sta + i) % STA}, device_id_type=MESH)
     sg = sign_rows()
 
     def beams(part, _):
@@ -419,7 +442,6 @@
     lax.fori_loop(0, CH, spectra, 0)
 
     pl.semaphore_wait(col_sem, STA - 1)
-    x_hi, z, core = sub // 8, (sub // 2) % 4, sub % 2
     x_lo, yh, jh_own = sta // 4, (sta // 2) % 2, sta % 2
 
     def group(i, _):
@@ -551,6 +573,7 @@
             pltpu.VMEM((128, 1, 128), F32),
             pltpu.SemaphoreType.DMA((LOADS + 8,)),
             pltpu.SemaphoreType.REGULAR,
+            pltpu.SemaphoreType.REGULAR,
             pltpu.SemaphoreType.DMA,
             pltpu.SemaphoreType.DMA((CH,)),
             pltpu.SemaphoreType.DMA,

time: 67.7 us -> 61.6 us (0.910)
  Pallas kernels: 66.9 us -> 60.8 us
    pallas_call x1, Pallas kernels: 64.9 us -> 58.8 us  [shards(): pl.pallas_call(kernel, out_shape=(pltpu.VMEM((128, 2, 16, 128), jnp.int16...]
where the time goes in v5:
time: 61.6 us; the launch traced here: 61.4 us
  Pallas kernels  60.8 us (99%)
  between operations  0.64 us (1%)
    pallas_call x1, Pallas kernels, shards(): pl.pallas_call(kernel, out_shape=(pltpu.VMEM((128, 2, 16, 128), jnp.int16...  58.8 us
    pallas_call x1, Pallas kernels, shards(): pl.pallas_call(assemble, out_shape=(jax.ShapeDtypeStruct((4096, 128), F32...  1.97 us

profile of v5, /device:TPU:0, one launch (start us, length us, event | category | flops | bytes accessed | tf_op | source)
XLA Modules:
  0.0 61.4 jit_solution(5787799941172031887)
XLA Ops:
  0.6 58.8 %shard_map.104 = (s16[128,2,16,128]{3,2,1,0:T(8,128)(2,1)S(1)}, f32[128,1,128]{2,1,0:T(1,128)S(1)}) custom-call(s32[8]{0:T(128)} %d_hbm.1, s32[4]{0:T(128)} %bitcast.3, bf16[1,2,8,65536]{3,2,1,0:T(8,128)(2,1)} %x_hbm.1, bf16[1,2,32,64]{3,2,1,0:T(8,128)(2,1)} %bw_hbm.1, bf16[256,256]{1,0:T(8,128)(2,1)} %constant.10.clone.w1_hbm, ...), custom_call_target="tpu_custom_call" | custom-call | tf_op jit(solution)/shard_map/pallas_call | solution.py:540
  59.5 2.0 %shard_map.105 = (f32[4096,128]{1,0:T(8,128)}, f32[128,128]{1,0:T(8,128)}) custom-call(s16[128,2,16,128]{3,2,1,0:T(8,128)(2,1)S(1)} %get-tuple-element.6.q_ref, f32[128,1,128]{2,1,0:T(1,128)S(1)} %get-tuple-element.7.s_ref), custom_call_target="tpu_custom_call" | custom-call | tf_op jit(solution)/shard_map/pallas_call | solution.py:595

commit v6 on v5

--- a/solution.py
+++ b/solution.py
@@ -23,9 +23,10 @@
 
 MESH = pl.DeviceIdType.MESH
 TOP = 32767.0
+LOG_TOP = float(np.log2(32766.0))
 CH = 8
 LOADS = 4
-HEAD_START = 10
+HEAD_START = 12
 
 
 def dft_tables():
@@ -194,6 +195,19 @@
     return jnp.round(values * (TOP / top)), top * (1.0 / TOP)
 
 
+def pack(values):
+    top = jnp.maximum(jnp.max(jnp.abs(values), axis=(0, 1), keepdims=True), 1e-33)
+    power = jnp.ceil(jnp.log2(top) - LOG_TOP)
+    q = jnp.round(values * jnp.exp2(-power)).astype(jnp.int32)
+    return ((q[0:2] << 16) | (q[2:4] & 0xFFFF)).reshape(16, 128), power.reshape(1, 128).astype(jnp.int32)
+
+
+def unpack(block):
+    words = block[0:16].reshape(2, 8, 128)
+    q = jnp.concatenate([words >> 16, (words << 16) >> 16], axis=0)
+    return q.astype(F32) * jnp.exp2(block[16:17].astype(F32))
+
+
 def decode(ints):
     return ints.astype(jnp.int32).astype(F32)
 
@@ -298,16 +312,16 @@
             g_ref[here, j] = cmul(y[j], twb_ref[0, here, pl.ds(j, 1)], twb_ref[1, here, pl.ds(j, 1)], -sg)
 
 
-PLACES = ((0, 2, 1), (1, 0, 0), (0, 1, 0), (1, 3, 1), (0, 0, 1), (1, 2, 0), (0, 3, 0), (1, 1, 1), (0, 2, 0), (1, 0, 1), (0, 1, 1), (1, 3, 0), (0, 3, 1), (1, 1, 0), (1, 2, 1), (0, 0, 0))
+EARLY_Z, LATE_Z = (0, 1), (2, 3)
 
 
 def kernel(
     d_hbm, dm_hbm, x_hbm, bw_hbm, w1_hbm, w2_hbm, tws_hbm, twb_hbm, twi_hbm,
-    recv3, rscale3,
+    recv3,
     d_ref, dm_ref, bw_ref, x_ref, w1_ref, w2_ref, tws_ref, twb_ref, twi_ref,
     xf_ref, send1, recv1, w_ref, bm_ref, send2, scale2, recv2, rscale2, base_ref, h_ref, xs_ref, gt_ref, g_ref,
-    send3, scale3,
-    load_sem, answer_sem, col_sem, sem1, rsem1, sem2, rsem2, ssem2, rssem2, sem3, rsem3, ssem3, rssem3,
+    send3,
+    load_sem, answer_sem, col_sem, sem1, rsem1, sem2, rsem2, ssem2, rssem2, sem3, rsem3,
 ):
     sub, sta = lax.axis_index("sub"), lax.axis_index("sta")
     me = sub * STA + sta
@@ -444,28 +458,15 @@
     pl.semaphore_wait(col_sem, STA - 1)
     x_lo, yh, jh_own = sta // 4, (sta // 2) % 2, sta % 2
 
-    def group(i, _):
-        a0 = 4 * ((core + 1 - (i // 4) % 2) % 2) + 2 * ((x_lo + 1 - (i // 2) % 2) % 2) + (yh + 1 - i % 2) % 2
-        for jh in range(2):
-            y = dft8([g_ref[8 * k0 + a0, pl.ds(4 * jh, 4)] for k0 in range(8)], -sg)
-            for a1 in range(8):
-                d = 16 * a1 + 2 * a0 + jh
-                q, scale = encode(y[a1], (0, 1))
-                send3[d] = q.reshape(2, 16, 128).astype(jnp.int16)
-                scale3[d] = scale.reshape(1, 128) * (1.0 / N)
-
-        for dx, dz, dj in PLACES:
-            d = 64 * ((x_hi + dx) % 2) + 16 * ((z + dz) % 4) + 2 * a0 + (jh_own + dj) % 2
+    def group_of(i):
+        return 4 * ((core + 1 - i // 4) % 2) + 2 * ((x_lo + 1 - (i // 2) % 2) % 2) + (yh + 1 - i % 2) % 2
+
+    def copies(a0, planes):
+        for n, z_to in enumerate(planes * 4):
+            dx, dj = 1 - n // (2 * len(planes)), 1 - (n // len(planes)) % 2
+            d = 64 * ((x_hi + dx) % 2) + 16 * z_to + 2 * a0 + (jh_own + dj) % 2
 
             def go():
-                pltpu.make_async_remote_copy(
-                    src_ref=scale3.at[d],
-                    dst_ref=rscale3.at[me],
-                    send_sem=ssem3,
-                    recv_sem=rssem3.at[sub],
-                    device_id={"sub": d // STA, "sta": d % STA},
-                    device_id_type=MESH,
-                ).start()
                 pltpu.make_async_remote_copy(
                     src_ref=send3.at[d],
                     dst_ref=recv3.at[me],
@@ -475,41 +476,51 @@
                     device_id_type=MESH,
                 ).start()
 
-            if dx or dz or dj:
+            if dx or dj:
                 go()
             else:
                 pl.when(d != me)(go)
 
                 @pl.when(d == me)
                 def _():
-                    pltpu.make_async_copy(scale3.at[me], rscale3.at[me], rssem3.at[sub]).start()
                     pltpu.make_async_copy(send3.at[me], recv3.at[me], rsem3.at[sub]).start()
 
+    def group(i, _):
+        a0 = group_of(i)
+        for jh in range(2):
+            y = dft8([g_ref[8 * k0 + a0, pl.ds(4 * jh, 4)] for k0 in range(8)], -sg)
+            for a1 in range(8):
+                d = 16 * a1 + 2 * a0 + jh
+                send3[d, 0:16], send3[d, 16:17] = pack(y[a1] * (1.0 / N))
+        copies(a0, EARLY_Z)
         return 0
 
     lax.fori_loop(0, 8, group, 0)
+
+    def rest(i, _):
+        copies(group_of(i), LATE_Z)
+        return 0
+
+    lax.fori_loop(0, 8, rest, 0)
 
     for s in range(SUB):
         block = recv3.at[pl.ds(s * STA, STA)]
         pltpu.make_async_copy(block, block, rsem3.at[s]).wait()
-        block = rscale3.at[pl.ds(s * STA, STA)]
-        pltpu.make_async_copy(block, block, rssem3.at[s]).wait()
     others = pl.ds(0, STA - 1)
     pltpu.make_async_copy(send1.at[others], send1.at[others], sem1).wait()
     pltpu.make_async_copy(send2.at[others], send2.at[others], sem2).wait()
     pltpu.make_async_copy(scale2.at[others], scale2.at[others], ssem2).wait()
     others = pl.ds(0, SUB * STA - 1)
     pltpu.make_async_copy(send3.at[others], send3.at[others], sem3).wait()
-    pltpu.make_async_copy(scale3.at[others], scale3.at[others], ssem3).wait()
-
-
-def assemble(q_ref, s_ref, out_hbm, int_ref, out_ref, acc_ref, out_sem):
+
+
+def assemble(q_ref, out_hbm, int_ref, out_ref, acc_ref, out_sem):
     acc_ref[...] = jnp.zeros_like(acc_ref)
 
     def one(s, _):
         for sta in range(STA):
             src = s * STA + sta
-            v = decode(q_ref[src].reshape(32, 128)).reshape(4, 8, 128) * s_ref[src]
+            v = unpack(q_ref[src])
             acc_ref[sta] += v * v
             for j4 in range(4):
                 for ri in range(2):
@@ -537,14 +548,11 @@
 def shards(voltages, beam_weights, station_delays, dm_index):
     w1, w2 = dft_tables()
     big, small, inner = twist_tables()
-    moved, scales = pl.pallas_call(
+    moved = pl.pallas_call(
         kernel,
-        out_shape=(
-            pltpu.VMEM((128, 2, 16, 128), jnp.int16),
-            pltpu.VMEM((128, 1, 128), F32),
-        ),
+        out_shape=pltpu.VMEM((128, 17, 128), jnp.int32),
         in_specs=[HBM] * 9,
-        out_specs=(ANY, ANY),
+        out_specs=ANY,
         scratch_shapes=[
             pltpu.SMEM((8,), jnp.int32),
             pltpu.SMEM((4,), jnp.int32),
@@ -569,8 +577,7 @@
             pltpu.VMEM((512, 256), BF16),
             pltpu.VMEM((8, 8, 8, 128), F32),
             pltpu.VMEM((64, 8, 8, 128), F32),
-            pltpu.VMEM((128, 2, 16, 128), jnp.int16),
-            pltpu.VMEM((128, 1, 128), F32),
+            pltpu.VMEM((128, 17, 128), jnp.int32),
             pltpu.SemaphoreType.DMA((LOADS + 8,)),
             pltpu.SemaphoreType.REGULAR,
             pltpu.SemaphoreType.REGULAR,
@@ -580,8 +587,6 @@
             pltpu.SemaphoreType.DMA((CH,)),
             pltpu.SemaphoreType.DMA,
             pltpu.SemaphoreType.DMA((CH,)),
-            pltpu.SemaphoreType.DMA,
-            pltpu.SemaphoreType.DMA((SUB,)),
             pltpu.SemaphoreType.DMA,
             pltpu.SemaphoreType.DMA((SUB,)),
         ],
@@ -595,7 +600,7 @@
     out, power = pl.pallas_call(
         assemble,
         out_shape=(jax.ShapeDtypeStruct((4096, 128), F32), jax.ShapeDtypeStruct((128, 128), F32)),
-        in_specs=[VM, VM],
+        in_specs=[VM],
         out_specs=(ANY, VM),
         scratch_shapes=[
             pltpu.VMEM((4096, 128), F32),
@@ -603,7 +608,7 @@
             pltpu.SemaphoreType.DMA,
         ],
         compiler_params=pltpu.CompilerParams(vmem_limit_bytes=16 * 1024 * 1024),
-    )(moved, scales)
+    )(moved)
     return out.reshape(16, 2, 32, 1, 512), power.reshape(32, 1, 512)
 
 

time: 61.6 us -> 60.2 us (0.977)
  Pallas kernels: 60.8 us -> 59.4 us
    pallas_call x1, Pallas kernels: 58.8 us -> 57.4 us  [shards(): pl.pallas_call(kernel, out_shape=pltpu.VMEM((128, 17, 128), jnp.int32), i...]
where the time goes in v6:
time: 60.2 us; the launch traced here: 60.1 us
  Pallas kernels  59.4 us (99%)
  between operations  0.64 us (1%)
    pallas_call x1, Pallas kernels, shards(): pl.pallas_call(kernel, out_shape=pltpu.VMEM((128, 17, 128), jnp.int32), i...  57.4 us
    pallas_call x1, Pallas kernels, shards(): pl.pallas_call(assemble, out_shape=(jax.ShapeDtypeStruct((4096, 128), F32...  1.99 us

profile of v6, /device:TPU:0, one launch (start us, length us, event | category | flops | bytes accessed | tf_op | source)
XLA Modules:
  0.0 60.1 jit_solution(3772840730545455308)
XLA Ops:
  0.6 57.4 %shard_map.104.q_ref = s32[128,17,128]{2,1,0:T(8,128)S(1)} custom-call(s32[8]{0:T(128)} %d_hbm.1, s32[4]{0:T(128)} %bitcast.3, bf16[1,2,8,65536]{3,2,1,0:T(8,128)(2,1)} %x_hbm.1, bf16[1,2,32,64]{3,2,1,0:T(8,128)(2,1)} %bw_hbm.1, bf16[256,256]{1,0:T(8,128)(2,1)} %constant.10.clone.w1_hbm, bf16[128,256]{1,0:T(8,128)(2,1)} %constant.11.clone.w2_hbm, ...), custom_call_target="tpu_custom_call" | custom-call | tf_op jit(solution)/shard_map/pallas_call | solution.py:551
  58.1 2.0 %shard_map.105 = (f32[4096,128]{1,0:T(8,128)}, f32[128,128]{1,0:T(8,128)}) custom-call(s32[128,17,128]{2,1,0:T(8,128)S(1)} %shard_map.104.q_ref), custom_call_target="tpu_custom_call" | custom-call | tf_op jit(solution)/shard_map/pallas_call | solution.py:600

commit v7 on v6

--- a/solution.py
+++ b/solution.py
@@ -22,11 +22,11 @@
 
 
 MESH = pl.DeviceIdType.MESH
-TOP = 32767.0
 LOG_TOP = float(np.log2(32766.0))
 CH = 8
-LOADS = 4
-HEAD_START = 12
+LOADS = 8
+QUARTER = LOADS // 4
+HEAD_START = 13
 
 
 def dft_tables():
@@ -96,19 +96,13 @@
             t = piece * per + i * 8 + u
             col = pl.multiple_of(t * 128, 128)
             for ri in range(2):
-                xf_ref[ri, t + 128] = x_ref[0, ri, :, pl.ds(col, 128)].astype(F32)
+                v = x_ref[0, ri, :, pl.ds(col, 128)].astype(F32)
+                xf_ref[ri, t + 128] = v
+                if piece >= LOADS - QUARTER:
+                    xf_ref[ri, t - 384] = v
         return 0
 
     lax.fori_loop(0, per // 8, body, 0)
-
-
-def wrap_voltages(xf_ref):
-    def wrap(i, _):
-        for ri in range(2):
-            xf_ref[ri, pl.ds(i * 8, 8)] = xf_ref[ri, pl.ds(i * 8 + 512, 8)]
-        return 0
-
-    lax.fori_loop(0, 16, wrap, 0, unroll=4)
 
 
 def delay_setup(d_ref):
@@ -123,7 +117,7 @@
     return starts, [row == r for r in range(8)], (lane - fine + 128) % 128, lane >= fine
 
 
-def delay_rows(setup, xf_ref, out_ref, a0):
+def delay_rows(setup, xf_ref, out_ref, a0, low=0, high=8):
     starts, masks, index, keep = setup
 
     def body(a1, _):
@@ -140,7 +134,7 @@
             out_ref[j, :, pl.ds(col, 128)] = jnp.concatenate([done[0][j], done[1][j]], axis=0).astype(BF16)
         return 0
 
-    lax.fori_loop(0, 8, body, 0, unroll=2)
+    lax.fori_loop(low, high, body, 0, unroll=2)
 
 
 def one_hot(shape, hit):
@@ -189,30 +183,32 @@
     lax.fori_loop(0, 4, body, 0, unroll=4)
 
 
-def encode(values, axes):
-    top = jnp.max(jnp.abs(values), axis=axes, keepdims=True)
-    top = jnp.maximum(top, 1e-33)
-    return jnp.round(values * (TOP / top)), top * (1.0 / TOP)
+def power_scale(top, axes):
+    top = jnp.maximum(jnp.max(top, axis=axes, keepdims=True), 1e-33)
+    power = jnp.ceil(jnp.log2(top) - LOG_TOP)
+    return jnp.exp2(-power), power.astype(jnp.int32)
+
+
+def two_in_one(high, low):
+    return (jnp.round(high).astype(jnp.int32) << 16) | (jnp.round(low).astype(jnp.int32) & 0xFFFF)
+
+
+def one_of_two(words):
+    return (words >> 16).astype(F32), ((words << 16) >> 16).astype(F32)
 
 
 def pack(values):
-    top = jnp.maximum(jnp.max(jnp.abs(values), axis=(0, 1), keepdims=True), 1e-33)
-    power = jnp.ceil(jnp.log2(top) - LOG_TOP)
-    q = jnp.round(values * jnp.exp2(-power)).astype(jnp.int32)
-    return ((q[0:2] << 16) | (q[2:4] & 0xFFFF)).reshape(16, 128), power.reshape(1, 128).astype(jnp.int32)
+    factor, power = power_scale(jnp.abs(values), (0, 1))
+    q = values * factor
+    return two_in_one(q[0:2], q[2:4]).reshape(16, 128), power.reshape(1, 128)
 
 
 def unpack(block):
-    words = block[0:16].reshape(2, 8, 128)
-    q = jnp.concatenate([words >> 16, (words << 16) >> 16], axis=0)
-    return q.astype(F32) * jnp.exp2(block[16:17].astype(F32))
-
-
-def decode(ints):
-    return ints.astype(jnp.int32).astype(F32)
-
-
-def outer_and_encode(bm_ref, k0, sta, twb_ref, sg, q_ref, s_ref):
+    high, low = one_of_two(block[0:16].reshape(2, 8, 128))
+    return jnp.concatenate([high, low], axis=0) * jnp.exp2(block[16:17].astype(F32))
+
+
+def outer_and_encode(bm_ref, k0, sta, twb_ref, sg, q_ref):
     for g in range(4):
         at = pl.ds(2 * g, 2)
         y = dft8([bm_ref[8 * i + k0, at] for i in range(8)], sg)
@@ -220,9 +216,10 @@
         for k1 in range(8):
             k = 8 * k0 + k1
             out.append(cmul(y[k1], twb_ref[0, k, pl.ds(sta, 1)], twb_ref[1, k, pl.ds(sta, 1)], sg))
-        q, scale = encode(jnp.stack(out, axis=1), (1, 2))
-        q_ref[at, pl.ds(4 * k0, 4)] = q.reshape(2, 4, 16, 128).astype(jnp.int16)
-        s_ref[at, k0] = scale.reshape(2, 1, 128)
+        factor, power = power_scale(functools.reduce(jnp.maximum, [jnp.abs(v) for v in out]), 1)
+        for m in range(4):
+            q_ref[at, k0, 8 * m : 8 * m + 8] = two_in_one(out[2 * m] * factor, out[2 * m + 1] * factor)
+        q_ref[at, k0, 32:33] = power
 
 
 def chirp_table(dm_ref, base_ref, h_ref, first, last):
@@ -270,9 +267,10 @@
     lax.fori_loop(first * 8, last * 8, body, 0)
 
 
-def middle(k0, r_ref, rs_ref, h_ref, w1_ref, w2_ref, tws_ref, twb_ref, xs_ref, gt_ref, g_ref, sg):
+def middle(k0, r_ref, h_ref, w1_ref, w2_ref, tws_ref, twb_ref, xs_ref, gt_ref, g_ref, sg):
+    scales = [jnp.exp2(r_ref[j, k0, 32:33].astype(F32)) for j in range(8)]
     for m in range(4):
-        x = [decode(r_ref[j, k0 * 4 + m]).reshape(2, 8, 128) * rs_ref[j, k0] for j in range(8)]
+        x = [jnp.stack(one_of_two(r_ref[j, k0, 8 * m : 8 * m + 8])) * scales[j] for j in range(8)]
         y = dft8(x, sg)
         for kj in range(8):
             v = y[kj]
@@ -319,9 +317,9 @@
     d_hbm, dm_hbm, x_hbm, bw_hbm, w1_hbm, w2_hbm, tws_hbm, twb_hbm, twi_hbm,
     recv3,
     d_ref, dm_ref, bw_ref, x_ref, w1_ref, w2_ref, tws_ref, twb_ref, twi_ref,
-    xf_ref, send1, recv1, w_ref, bm_ref, send2, scale2, recv2, rscale2, base_ref, h_ref, xs_ref, gt_ref, g_ref,
+    xf_ref, send1, recv1, w_ref, bm_ref, send2, recv2, base_ref, h_ref, xs_ref, gt_ref, g_ref,
     send3,
-    load_sem, answer_sem, col_sem, sem1, rsem1, sem2, rsem2, ssem2, rssem2, sem3, rsem3,
+    load_sem, answer_sem, col_sem, sem1, rsem1, sem2, rsem2, sem3, rsem3,
 ):
     sub, sta = lax.axis_index("sub"), lax.axis_index("sta")
     me = sub * STA + sta
@@ -339,7 +337,8 @@
             ]
         )
     ]
-    for t in tables[:1] + x_loads + tables[1:]:
+    order = [(i - QUARTER) % LOADS for i in range(LOADS)]
+    for t in tables[:1] + [x_loads[i] for i in order] + tables[1:2]:
         t.start()
 
     barrier = pltpu.get_barrier_semaphore()
@@ -356,15 +355,17 @@
         return 0
 
     lax.fori_loop(rank + 1, SUB, greet, 0)
-    for i in range(LOADS):
-        x_loads[i].wait()
-        unpack_voltages(x_ref, xf_ref, i)
-    wrap_voltages(xf_ref)
+    def load(pieces):
+        for i in pieces:
+            x_loads[i].wait()
+            unpack_voltages(x_ref, xf_ref, i)
+
     tables[0].wait()
     setup = delay_setup(d_ref)
-
-    def first(part):
-        cols = pl.ds(pl.multiple_of(part * 1024, 1024), 1024)
+    load(order[:QUARTER])
+
+    def first(part, start, size):
+        cols = pl.ds(pl.multiple_of(start, size), size)
         for i in range(1, STA):
             d = (sta + i) % STA
             pltpu.make_async_remote_copy(
@@ -380,9 +381,12 @@
     tables[1].wait()
     late = HEAD_START * (1 - (sub % 2))
     chirp_table(dm_ref, base_ref, h_ref, 0, late)
+    load(order[QUARTER:])
     delay_rows(setup, xf_ref, send1, 0)
     pl.semaphore_wait(barrier, STA - 1 + rank)
-    first(0)
+    first(0, 0, 1024)
+    for t in tables[2:]:
+        t.start()
 
     def answer(r, _):
         pl.semaphore_signal(answer_sem, inc=1, device_id=column(r), device_id_type=MESH)
@@ -392,7 +396,7 @@
 
     def more(part, _):
         delay_rows(setup, xf_ref, send1, part)
-        first(part)
+        first(part, part * 1024, 1024)
         return 0
 
     lax.fori_loop(1, CH, more, 0)
@@ -419,37 +423,25 @@
     lax.fori_loop(0, CH, beams, 0)
 
     def second(part, _):
-        outer_and_encode(bm_ref, part, sta, twb_ref, sg, send2, scale2)
-        rows = pl.ds(part * 4, 4)
+        outer_and_encode(bm_ref, part, sta, twb_ref, sg, send2)
         for i in range(1, STA):
             d = (sta + i) % STA
             pltpu.make_async_remote_copy(
-                src_ref=scale2.at[d, part],
-                dst_ref=rscale2.at[sta, part],
-                send_sem=ssem2,
-                recv_sem=rssem2.at[part],
-                device_id={"sub": sub, "sta": d},
-                device_id_type=MESH,
-            ).start()
-            pltpu.make_async_remote_copy(
-                src_ref=send2.at[d, rows],
-                dst_ref=recv2.at[sta, rows],
+                src_ref=send2.at[d, part],
+                dst_ref=recv2.at[sta, part],
                 send_sem=sem2,
                 recv_sem=rsem2.at[part],
                 device_id={"sub": sub, "sta": d},
                 device_id_type=MESH,
             ).start()
-        pltpu.make_async_copy(scale2.at[sta, part], rscale2.at[sta, part], rssem2.at[part]).start()
-        pltpu.make_async_copy(send2.at[sta, rows], recv2.at[sta, rows], rsem2.at[part]).start()
+        pltpu.make_async_copy(send2.at[sta, part], recv2.at[sta, part], rsem2.at[part]).start()
         return 0
 
     lax.fori_loop(0, CH, second, 0)
 
     def spectra(part, _):
-        rows = pl.ds(part * 4, 4)
-        pltpu.make_async_copy(rscale2.at[:, part], rscale2.at[:, part], rssem2.at[part]).wait()
-        pltpu.make_async_copy(recv2.at[:, rows], recv2.at[:, rows], rsem2.at[part]).wait()
-        middle(part, recv2, rscale2, h_ref, w1_ref, w2_ref, tws_ref, twb_ref, xs_ref, gt_ref, g_ref, sg)
+        pltpu.make_async_copy(recv2.at[:, part], recv2.at[:, part], rsem2.at[part]).wait()
+        middle(part, recv2, h_ref, w1_ref, w2_ref, tws_ref, twb_ref, xs_ref, gt_ref, g_ref, sg)
         inner_pass(g_ref, part, twi_ref, -sg)
         return 0
 
@@ -509,7 +501,6 @@
     others = pl.ds(0, STA - 1)
     pltpu.make_async_copy(send1.at[others], send1.at[others], sem1).wait()
     pltpu.make_async_copy(send2.at[others], send2.at[others], sem2).wait()
-    pltpu.make_async_copy(scale2.at[others], scale2.at[others], ssem2).wait()
     others = pl.ds(0, SUB * STA - 1)
     pltpu.make_async_copy(send3.at[others], send3.at[others], sem3).wait()
 
@@ -568,10 +559,8 @@
             pltpu.VMEM((8, 16, 8192), BF16),
             pltpu.VMEM((64, 128), BF16),
             pltpu.VMEM((64, 8, 8, 128), F32),
-            pltpu.VMEM((8, 32, 16, 128), jnp.int16),
-            pltpu.VMEM((8, CH, 1, 128), F32),
-            pltpu.VMEM((8, 32, 16, 128), jnp.int16),
-            pltpu.VMEM((8, CH, 1, 128), F32),
+            pltpu.VMEM((8, CH, 33, 128), jnp.int32),
+            pltpu.VMEM((8, CH, 33, 128), jnp.int32),
             pltpu.VMEM((512, 128), F32),
             pltpu.VMEM((512, 8, 128), F32),
             pltpu.VMEM((512, 256), BF16),
@@ -581,8 +570,6 @@
             pltpu.SemaphoreType.DMA((LOADS + 8,)),
             pltpu.SemaphoreType.REGULAR,
             pltpu.SemaphoreType.REGULAR,
-            pltpu.SemaphoreType.DMA,
-            pltpu.SemaphoreType.DMA((CH,)),
             pltpu.SemaphoreType.DMA,
             pltpu.SemaphoreType.DMA((CH,)),
             pltpu.SemaphoreType.DMA,

time: 60.2 us -> 59.6 us (0.990)
  Pallas kernels: 59.4 us -> 58.4 us
    pallas_call x1, Pallas kernels: 57.4 us -> 56.4 us  [shards(): pl.pallas_call(kernel, out_shape=pltpu.VMEM((128, 17, 128), jnp.int32), i...]
where the time goes in v7:
time: 59.6 us; the launch traced here: 59 us
  Pallas kernels  58.4 us (98%)
  between operations  0.64 us (1%)
    pallas_call x1, Pallas kernels, shards(): pl.pallas_call(kernel, out_shape=pltpu.VMEM((128, 17, 128), jnp.int32), i...  56.4 us
    pallas_call x1, Pallas kernels, shards(): pl.pallas_call(assemble, out_shape=(jax.ShapeDtypeStruct((4096, 128), F32...  1.99 us

profile of v7, /device:TPU:0, one launch (start us, length us, event | category | flops | bytes accessed | tf_op | source)
XLA Modules:
  0.0 59.0 jit_solution(16631776719577652447)
XLA Ops:
  0.6 56.4 %shard_map.104.q_ref = s32[128,17,128]{2,1,0:T(8,128)S(1)} custom-call(s32[8]{0:T(128)} %d_hbm.1, s32[4]{0:T(128)} %bitcast.3, bf16[1,2,8,65536]{3,2,1,0:T(8,128)(2,1)} %x_hbm.1, bf16[1,2,32,64]{3,2,1,0:T(8,128)(2,1)} %bw_hbm.1, bf16[256,256]{1,0:T(8,128)(2,1)} %constant.10.clone.w1_hbm, bf16[128,256]{1,0:T(8,128)(2,1)} %constant.11.clone.w2_hbm, ...), custom_call_target="tpu_custom_call" | custom-call | tf_op jit(solution)/shard_map/pallas_call | solution.py:542
  57.0 2.0 %shard_map.105 = (f32[4096,128]{1,0:T(8,128)}, f32[128,128]{1,0:T(8,128)}) custom-call(s32[128,17,128]{2,1,0:T(8,128)S(1)} %shard_map.104.q_ref), custom_call_target="tpu_custom_call" | custom-call | tf_op jit(solution)/shard_map/pallas_call | solution.py:587

commit v8 on v7

--- a/solution.py
+++ b/solution.py
@@ -22,7 +22,7 @@
 
 
 MESH = pl.DeviceIdType.MESH
-LOG_TOP = float(np.log2(32766.0))
+LOG_TOP = float(np.log2(32640.0))
 CH = 8
 LOADS = 8
 QUARTER = LOADS // 4

time: 59.6 us -> 59.6 us (level)
  no operation moved by 1% of the time
where the time goes in v8:
time: 59.6 us; the launch traced here: 59 us
  Pallas kernels  58.3 us (98%)
  between operations  0.64 us (1%)
    pallas_call x1, Pallas kernels, shards(): pl.pallas_call(kernel, out_shape=pltpu.VMEM((128, 17, 128), jnp.int32), i...  56.3 us
    pallas_call x1, Pallas kernels, shards(): pl.pallas_call(assemble, out_shape=(jax.ShapeDtypeStruct((4096, 128), F32...  1.99 us

profile of v8, /device:TPU:0, one launch (start us, length us, event | category | flops | bytes accessed | tf_op | source)
XLA Modules:
  0.0 59.0 jit_solution(3617463866817864871)
XLA Ops:
  0.6 56.3 %shard_map.104.q_ref = s32[128,17,128]{2,1,0:T(8,128)S(1)} custom-call(s32[8]{0:T(128)} %d_hbm.1, s32[4]{0:T(128)} %bitcast.3, bf16[1,2,8,65536]{3,2,1,0:T(8,128)(2,1)} %x_hbm.1, bf16[1,2,32,64]{3,2,1,0:T(8,128)(2,1)} %bw_hbm.1, bf16[256,256]{1,0:T(8,128)(2,1)} %constant.10.clone.w1_hbm, bf16[128,256]{1,0:T(8,128)(2,1)} %constant.11.clone.w2_hbm, ...), custom_call_target="tpu_custom_call" | custom-call | tf_op jit(solution)/shard_map/pallas_call | solution.py:542
  57.0 2.0 %shard_map.105 = (f32[4096,128]{1,0:T(8,128)}, f32[128,128]{1,0:T(8,128)}) custom-call(s32[128,17,128]{2,1,0:T(8,128)S(1)} %shard_map.104.q_ref), custom_call_target="tpu_custom_call" | custom-call | tf_op jit(solution)/shard_map/pallas_call | solution.py:587

commit v9 on v8

--- a/solution.py
+++ b/solution.py
@@ -134,7 +134,7 @@
             out_ref[j, :, pl.ds(col, 128)] = jnp.concatenate([done[0][j], done[1][j]], axis=0).astype(BF16)
         return 0
 
-    lax.fori_loop(low, high, body, 0, unroll=2)
+    lax.fori_loop(low, high, body, 0, unroll=4)
 
 
 def one_hot(shape, hit):
@@ -385,9 +385,6 @@
     delay_rows(setup, xf_ref, send1, 0)
     pl.semaphore_wait(barrier, STA - 1 + rank)
     first(0, 0, 1024)
-    for t in tables[2:]:
-        t.start()
-
     def answer(r, _):
         pl.semaphore_signal(answer_sem, inc=1, device_id=column(r), device_id_type=MESH)
         return 0
@@ -400,6 +397,8 @@
         return 0
 
     lax.fori_loop(1, CH, more, 0)
+    for t in tables[2:]:
+        t.start()
 
     for t in tables[2:]:
         t.wait()

time: 59.6 us -> 59.7 us (level)
  no operation moved by 1% of the time
where the time goes in v9:
time: 59.7 us; the launch traced here: 59 us
  Pallas kernels  58.3 us (98%)
  between operations  0.64 us (1%)
    pallas_call x1, Pallas kernels, shards(): pl.pallas_call(kernel, out_shape=pltpu.VMEM((128, 17, 128), jnp.int32), i...  56.3 us
    pallas_call x1, Pallas kernels, shards(): pl.pallas_call(assemble, out_shape=(jax.ShapeDtypeStruct((4096, 128), F32...  1.99 us

profile of v9, /device:TPU:0, one launch (start us, length us, event | category | flops | bytes accessed | tf_op | source)
XLA Modules:
  0.0 59.0 jit_solution(5775054713601858713)
XLA Ops:
  0.6 56.3 %shard_map.104.q_ref = s32[128,17,128]{2,1,0:T(8,128)S(1)} custom-call(s32[8]{0:T(128)} %d_hbm.1, s32[4]{0:T(128)} %bitcast.3, bf16[1,2,8,65536]{3,2,1,0:T(8,128)(2,1)} %x_hbm.1, bf16[1,2,32,64]{3,2,1,0:T(8,128)(2,1)} %bw_hbm.1, bf16[256,256]{1,0:T(8,128)(2,1)} %constant.10.clone.w1_hbm, bf16[128,256]{1,0:T(8,128)(2,1)} %constant.11.clone.w2_hbm, ...), custom_call_target="tpu_custom_call" | custom-call | tf_op jit(solution)/shard_map/pallas_call | solution.py:541
  57.0 2.0 %shard_map.105 = (f32[4096,128]{1,0:T(8,128)}, f32[128,128]{1,0:T(8,128)}) custom-call(s32[128,17,128]{2,1,0:T(8,128)S(1)} %shard_map.104.q_ref), custom_call_target="tpu_custom_call" | custom-call | tf_op jit(solution)/shard_map/pallas_call | solution.py:586
